TPU v7x, 32 devices: a whole 2x2x4 slice. The times are simulated.
32 devices in a mesh: sfc: 8 (over z, x), grp: 4 (over y, core).
Axes of the slice: x: 2, y: 2, z: 4, core: 2. Of those that a mesh axis runs over, the one named last changes fastest.
Arguments:
- source: float32 [32, 16, 1024], P('sfc', None, 'grp'), may hold values from -8 to 8
- layer_counts: int32 [8], P('sfc'), may hold values from 1 to 4, 21 in all
Outputs:
- solution: float32 [32, 16, 1024], P('sfc', None, 'grp')
- residual: float32 [32, 16, 1024], P('sfc', None, 'grp')
- direction: float32 [32, 16, 1024], P('sfc', None, 'grp')
Inputs may be any that keep to these rules, and one draw needn't show every extreme that they name: `layer_counts`: each entry counts the live leading slots of that index of sfc; they sum to 21, and at least one entry equals 4.
All inputs are finite; a program needn't handle non-finite values. No bound on the sum of `layer_counts` on one device may be relied on, other than what follows from the above.
Results may differ from a plain program's by a relative error of at most 0.00011.
Values sent between devices are 32-bit elements; how exact they have to be, the bound alone decides.
No kernel may reach another device: no remote copies, remote signals or barrier semaphores. Data moves between devices by JAX's collectives and lax.ppermute only.
A program may use at most 64 MiB of HBM per device.

v0:
```python
import jax
import jax.numpy as jnp
from jax import lax
from jax.sharding import PartitionSpec as P

PRE_SWEEPS = 2
POST_SWEEPS = 2
COARSE_SWEEPS = 4


OMEGA = 2.0 / 3.0


def padded_2(cells, sides, width):
    for axis, dim in sides:
        count = lax.axis_size(axis)
        ends = count - 1
        head = lax.slice_in_dim(cells, 0, width, axis=dim)
        tail = lax.slice_in_dim(cells, cells.shape[dim] - width, cells.shape[dim], axis=dim)
        cells = jnp.concatenate(
            [
                lax.ppermute(tail, axis, [(i, (i + 1) % count) for i in range(ends)]),
                cells,
                lax.ppermute(head, axis, [((i + 1) % count, i) for i in range(ends)]),
            ],
            axis=dim,
        )
    return cells


def laplace(field, count, edge, outer_faces, side_faces):
    planes, width = field.shape
    plane = lax.broadcasted_iota(jnp.int32, (planes, 1), 0)
    last_index = count * edge - 1
    last = lax.dynamic_slice_in_dim(field, last_index, 1, 0)
    ends = outer_faces(jnp.concatenate([field[:1], last], axis=0))
    below = jnp.concatenate([ends[:1], field[:-1]], axis=0)
    above = jnp.concatenate([field[1:], jnp.zeros((1, width), jnp.float32)], axis=0)
    above = above + jnp.where(plane == last_index, ends[3:], 0.0)
    south, north = side_faces(
        jnp.concatenate([field[:, :edge], field[:, width - edge :]], axis=1), edge
    )
    north_rows = jnp.concatenate([field[:, edge:], north], axis=1)
    south_rows = jnp.concatenate([south, field[:, : width - edge]], axis=1)
    column = lax.broadcasted_iota(jnp.int32, (1, width), 1) % edge
    pad_col = jnp.zeros((planes, 1), jnp.float32)
    up_z = jnp.where(column != edge - 1, jnp.concatenate([field[:, 1:], pad_col], axis=1), 0.0)
    down_z = jnp.where(column != 0, jnp.concatenate([pad_col, field[:, :-1]], axis=1), 0.0)
    total = 6.0 * field - below - above - north_rows - south_rows - up_z - down_z
    return jnp.where(plane < count * edge, total, 0.0)


def padded_laplace(field, edge):
    planes, width = field.shape
    zero_plane = jnp.zeros((1, width), jnp.float32)
    below = jnp.concatenate([zero_plane, field[:-1]], axis=0)
    above = jnp.concatenate([field[1:], zero_plane], axis=0)
    pad_rows = jnp.zeros((planes, edge), jnp.float32)
    north_rows = jnp.concatenate([field[:, edge:], pad_rows], axis=1)
    south_rows = jnp.concatenate([pad_rows, field[:, : width - edge]], axis=1)
    column = lax.broadcasted_iota(jnp.int32, (1, width), 1) % edge
    pad_col = jnp.zeros((planes, 1), jnp.float32)
    up_z = jnp.where(column != edge - 1, jnp.concatenate([field[:, 1:], pad_col], axis=1), 0.0)
    down_z = jnp.where(column != 0, jnp.concatenate([pad_col, field[:, :-1]], axis=1), 0.0)
    return 6.0 * field - below - above - north_rows - south_rows - up_z - down_z


def deep_extend(stacked, count, edge, depth):
    kinds, planes, width = stacked.shape
    last = lax.dynamic_slice_in_dim(stacked, count * edge - depth, depth, 1)
    ends = jnp.concatenate([stacked[:, :depth], last], axis=1)
    got = padded_2(ends, (("sfc", 1),), depth)
    blank = jnp.zeros((kinds, depth, width), jnp.float32)
    extended = jnp.concatenate([got[:, :depth], stacked, blank], axis=1)
    extended = lax.dynamic_update_slice_in_dim(
        extended, got[:, 3 * depth :], depth + count * edge, 1
    )
    span = depth * edge
    faces = jnp.concatenate([extended[:, :, :span], extended[:, :, width - span :]], axis=2)
    wide = padded_2(faces, (("grp", 2),), span)
    return jnp.concatenate([wide[:, :, :span], extended, wide[:, :, 3 * span :]], axis=2)


def deep_mask(count, edge, depth, planes, width):
    span = depth * edge
    sfc_index = lax.axis_index("sfc")
    grp_index = lax.axis_index("grp")
    sfc_last = lax.axis_size("sfc") - 1
    grp_last = lax.axis_size("grp") - 1
    plane = lax.broadcasted_iota(jnp.int32, (planes + 2 * depth, 1), 0)
    live_end = depth + count * edge
    plane_ok = (plane < depth) & (sfc_index > 0) | (plane >= depth) & (plane < live_end)
    plane_ok = plane_ok | (plane >= live_end) & (plane < live_end + depth) & (sfc_index < sfc_last)
    column = lax.broadcasted_iota(jnp.int32, (1, width + 2 * span), 1)
    column_ok = (column < span) & (grp_index > 0) | (column >= span) & (column < span + width)
    column_ok = column_ok | (column >= span + width) & (grp_index < grp_last)
    return plane_ok & column_ok


def trim_live(padded, count, edge, depth, planes, width):
    span = depth * edge
    inner = padded[depth : depth + planes, span : span + width]
    plane = lax.broadcasted_iota(jnp.int32, (planes, 1), 0)
    return jnp.where(plane < count * edge, inner, 0.0)


def fine_ends(ends):
    return padded_2(ends, (("sfc", 0),), 1)


def fine_sides(faces, edge):
    wide = padded_2(faces, (("grp", 1),), edge)
    return (wide[:, :edge], wide[:, 3 * edge :])


def coarse_ends(ends):
    return padded_2(ends, (("sfc", 0),), 1)


def coarse_sides(faces, edge):
    wide = padded_2(faces, (("grp", 1),), edge)
    return (wide[:, :edge], wide[:, 3 * edge :])


def fine_laplace(field, count, edge):
    return laplace(field, count, edge, fine_ends, fine_sides)


def restrict(field, half):
    planes = field.shape[0]
    blocks = field.reshape(planes // 2, 2, half, 2, half, 2)
    return 0.125 * jnp.sum(blocks, axis=(1, 3, 5)).reshape(planes // 2, half * half)


def prolong(coarse, half):
    planes = coarse.shape[0]
    blocks = coarse.reshape(planes, 1, half, 1, half, 1)
    blocks = jnp.broadcast_to(blocks, (planes, 2, half, 2, half, 2))
    return blocks.reshape(planes * 2, 4 * half * half)


def coarse_solve(coarse_rhs, count, half):
    coarse_step = OMEGA / 1.5
    correction = coarse_step * coarse_rhs
    for sweep in range(COARSE_SWEEPS - 1):
        applied = laplace(correction, count, half, coarse_ends, coarse_sides)
        correction = correction + coarse_step * (coarse_rhs - 0.25 * applied)
    return correction


def vcycle(rhs, count, edge):
    step = OMEGA / 6.0
    half = edge // 2
    planes, width = rhs.shape
    depth = max(PRE_SWEEPS, POST_SWEEPS)
    keeper = deep_mask(count, edge, depth, planes, width)
    padded_rhs = deep_extend(rhs[None], count, edge, depth)[0]
    padded_z = step * padded_rhs
    padded_z = jnp.where(
        keeper, padded_z + step * (padded_rhs - padded_laplace(padded_z, edge)), 0.0
    )
    padded_defect = padded_rhs - padded_laplace(padded_z, edge)
    smooth = trim_live(padded_z, count, edge, depth, planes, width)
    defect = trim_live(padded_defect, count, edge, depth, planes, width)
    correction = coarse_solve(restrict(defect, half), count, half)
    smooth = smooth + prolong(correction, half)
    both = deep_extend(jnp.stack([rhs, smooth]), count, edge, depth)
    padded_rhs = both[0]
    padded_z = both[1]
    for sweep in range(POST_SWEEPS):
        padded_z = jnp.where(
            keeper, padded_z + step * (padded_rhs - padded_laplace(padded_z, edge)), 0.0
        )
    return trim_live(padded_z, count, edge, depth, planes, width)


def shards(source, layer_counts):
    count = layer_counts[0]
    slots, edge, width = source.shape
    planes = slots * edge
    plane = lax.broadcasted_iota(jnp.int32, (planes, 1), 0)
    first_rhs = jnp.where(plane < count * edge, source.reshape(planes, width), 0.0)
    first_z = vcycle(first_rhs, count, edge)
    rz_value = lax.psum(jnp.sum(first_rhs * first_z), ("sfc", "grp"))
    image = fine_laplace(first_z, count, edge)
    curv = lax.psum(jnp.sum(first_z * image), ("sfc", "grp"))
    alpha = rz_value / curv
    solution = alpha * first_z
    residual = first_rhs - alpha * image
    next_z = vcycle(residual, count, edge)
    cross = lax.psum(jnp.sum(next_z * image), ("sfc", "grp"))
    direction = next_z - cross / curv * first_z
    shape = (slots, edge, width)
    return (solution.reshape(shape), residual.reshape(shape), direction.reshape(shape))


def solution(mesh):
    return jax.shard_map(
        shards,
        mesh=mesh,
        in_specs=(P("sfc", None, "grp"), P("sfc")),
        out_specs=(P("sfc", None, "grp"), P("sfc", None, "grp"), P("sfc", None, "grp")),
        check_vma=False,
    )
```

profile of v0, /device:TPU:0, one launch (start us, length us, event | category | flops | bytes accessed | tf_op | source)
XLA Modules:
  0.0 298.7 jit_solution(9715950964302466820)
XLA Ops:
  2.2 1.3 collective-permute-start.1
  4.5 5.5 %collective-permute-start = (f32[1,2,256]{2,1,0:T(2,128)S(1)}, f32[1,2,256]{2,1,0:T(2,128)S(1)}, u32[]{:S(2)}, u32[]{:S(2)}) collective-permute-start(f32[1,2,256]{2,1,0:T(2,128)S(1)} %fusion.88), channel_id=1, source_target_pairs={{0,4},{4,8},{8,12},{12,16},{16,20},{20,24},{24,28},{1,5},{5,9},{9,... | collective-permute-start | bytes 6152 | tf_op jit(solution)/shard_map/ppermute | solution.py:22
  14.2 3.9 %collective-permute-done.3 = f32[1,68,32]{2,1,0:T(8,128)S(1)} collective-permute-done((f32[1,68,32]{2,1,0:T(8,128)S(1)}, f32[1,68,32]{2,1,0:T(8,128)S(1)}, u32[]{:S(2)}, u32[]{:S(2)}) %collective-permute-start.3) | collective-permute-done | bytes 8736 | tf_op jit(solution)/shard_map/ppermute | solution.py:24
  19.1 5.6 %reshape.237 = f32[32,2,8,2,8,2]{5,4,3,2,1,0:T(8,128)} reshape(f32[64,256]{1,0:T(8,128)S(1)} %fusion.13) | data formatting | bytes 131072 | tf_op jit(solution)/shard_map/reshape | solution.py:131
  24.7 2.6 reduce_sum.45
  28.9 4.6 %collective-permute-start.7 = (f32[32,8]{0,1:T(8,128)S(1)}, f32[32,8]{0,1:T(8,128)S(1)}, u32[]{:S(2)}, u32[]{:S(2)}) collective-permute-start(f32[32,8]{0,1:T(8,128)S(1)} %get-tuple-element.142), channel_id=1, source_target_pairs={{0,1},{1,2},{2,3},{4,5},{5,6},{6,7},{8,9},{9,10},{10,11},{12,13},{... | collective-permute-start | bytes 3080 | tf_op jit(solution)/shard_map/ppermute | solution.py:22
  34.9 4.9 %collective-permute-start.4 = (f32[1,64]{0,1:T(8,128)S(1)}, f32[1,64]{0,1:T(8,128)S(1)}, u32[]{:S(2)}, u32[]{:S(2)}) collective-permute-start(f32[1,64]{0,1:T(8,128)S(1)} %constant_dynamic-slice_fusion.7), channel_id=1, source_target_pairs={{0,4},{4,8},{8,12},{12,16},{16,20},{20,24},{24,28},{1,5},{5,9},{9,... | collective-permute-start | bytes 776 | tf_op jit(solution)/shard_map/ppermute | solution.py:22
  40.1 1.3 collective-permute-done.4
  41.7 2.3 collective-permute-start.11
  44.0 1.3 collective-permute-start.10
  45.3 1.3 collective-permute-start.9
  46.6 5.7 %collective-permute-start.8 = (f32[1,64]{0,1:T(8,128)S(1)}, f32[1,64]{0,1:T(8,128)S(1)}, u32[]{:S(2)}, u32[]{:S(2)}) collective-permute-start(f32[1,64]{0,1:T(8,128)S(1)} %get-tuple-element.131), channel_id=1, source_target_pairs={{0,4},{4,8},{8,12},{12,16},{16,20},{20,24},{24,28},{1,5},{5,9},{9,... | collective-permute-start | bytes 776 | tf_op jit(solution)/shard_map/ppermute | solution.py:22
  52.4 1.4 collective-permute-done.8
  54.2 3.7 %collective-permute-start.15 = (f32[32,8]{0,1:T(8,128)S(1)}, f32[32,8]{0,1:T(8,128)S(1)}, u32[]{:S(2)}, u32[]{:S(2)}) collective-permute-start(f32[32,8]{0,1:T(8,128)S(1)} %get-tuple-element.126), channel_id=1, source_target_pairs={{0,1},{1,2},{2,3},{4,5},{5,6},{6,7},{8,9},{9,10},{10,11},{12,13},{... | collective-permute-start | bytes 3080 | tf_op jit(solution)/shard_map/ppermute | solution.py:22
  60.5 5.8 %collective-permute-start.12 = (f32[1,64]{0,1:T(8,128)S(1)}, f32[1,64]{0,1:T(8,128)S(1)}, u32[]{:S(2)}, u32[]{:S(2)}) collective-permute-start(f32[1,64]{0,1:T(8,128)S(1)} %get-tuple-element.121), channel_id=1, source_target_pairs={{0,4},{4,8},{8,12},{12,16},{16,20},{20,24},{24,28},{1,5},{5,9},{9,... | collective-permute-start | bytes 776 | tf_op jit(solution)/shard_map/ppermute | solution.py:22
  66.4 1.4 collective-permute-done.12
  68.1 2.4 broadcast_in_dim.409
  70.4 4.0 %reshape.238 = f32[64,256]{1,0:T(8,128)S(1)} reshape(f32[32,2,8,2,8,2]{5,4,3,2,1,0:T(8,128)} %broadcast_in_dim.409) | data formatting | bytes 131072 | tf_op jit(solution)/shard_map/reshape | solution.py:139
  74.6 4.8 %collective-permute-start.16 = (f32[2,2,256]{2,1,0:T(2,128)S(1)}, f32[2,2,256]{2,1,0:T(2,128)S(1)}, u32[]{:S(2)}, u32[]{:S(2)}) collective-permute-start(f32[2,2,256]{2,1,0:T(2,128)S(1)} %get-tuple-element.31), channel_id=1, source_target_pairs={{0,4},{4,8},{8,12},{12,16},{16,20},{20,24},{24,28},{1,5},{5,9},{9,... | collective-permute-start | bytes 12296 | tf_op jit(solution)/shard_map/ppermute | solution.py:22
  80.9 5.4 %collective-permute-done.17 = f32[2,2,256]{2,1,0:T(2,128)S(1)} collective-permute-done((f32[2,2,256]{2,1,0:T(2,128)S(1)}, f32[2,2,256]{2,1,0:T(2,128)S(1)}, u32[]{:S(2)}, u32[]{:S(2)}) %collective-permute-start.17) | collective-permute-done | bytes 4128 | tf_op jit(solution)/shard_map/ppermute | solution.py:24
  86.3 3.1 %collective-permute-start.18 = (f32[2,68,32]{2,1,0:T(8,128)S(1)}, f32[2,68,32]{2,1,0:T(8,128)S(1)}, u32[]{:S(2)}, u32[]{:S(2)}) collective-permute-start(f32[2,68,32]{2,1,0:T(8,128)S(1)} %get-tuple-element.24), channel_id=1, source_target_pairs={{0,1},{1,2},{2,3},{4,5},{5,6},{6,7},{8,9},{9,10},{10,11},{12,13},{... | collective-permute-start | bytes 52232 | tf_op jit(solution)/shard_map/ppermute | solution.py:22
  90.7 5.4 %collective-permute-done.19 = f32[2,68,32]{2,1,0:T(8,128)S(1)} collective-permute-done((f32[2,68,32]{2,1,0:T(8,128)S(1)}, f32[2,68,32]{2,1,0:T(8,128)S(1)}, u32[]{:S(2)}, u32[]{:S(2)}) %collective-permute-start.19) | collective-permute-done | bytes 17440 | tf_op jit(solution)/shard_map/ppermute | solution.py:24
  97.4 4.8 %collective-permute-start.20 = (f32[1,256]{1,0:T(1,128)S(1)}, f32[1,256]{1,0:T(1,128)S(1)}, u32[]{:S(2)}, u32[]{:S(2)}) collective-permute-start(f32[1,256]{1,0:T(1,128)S(1)} %get-tuple-element.84), channel_id=1, source_target_pairs={{0,4},{4,8},{8,12},{12,16},{16,20},{20,24},{24,28},{1,5},{5,9},{9,... | collective-permute-start | bytes 3080 | tf_op jit(solution)/shard_map/ppermute | solution.py:22
  104.9 5.3 %collective-permute-start.23 = (f32[64,16]{1,0:T(8,128)S(1)}, f32[64,16]{1,0:T(8,128)S(1)}, u32[]{:S(2)}, u32[]{:S(2)}) collective-permute-start(f32[64,16]{1,0:T(8,128)S(1)} %get-tuple-element.91), channel_id=1, source_target_pairs={{0,1},{1,2},{2,3},{4,5},{5,6},{6,7},{8,9},{9,10},{10,11},{12,13},{... | collective-permute-start | bytes 12296 | tf_op jit(solution)/shard_map/ppermute | solution.py:22
  111.7 45.1 %all-reduce.69 = (f32[]{:T(128)}, f32[]{:T(128)}) all-reduce(f32[]{:T(128)} %get-tuple-element.4, f32[]{:T(128)} %get-tuple-element.3), channel_id=1, replica_groups=mesh['sfc'=8,'grp'=4] {'sfc','grp'}, use_global_device_ids=true, to_apply=%region_2.3 | all-reduce | flops 2 | bytes 16 | tf_op jit(solution)/shard_map/psum | solution.py:184
  158.3 4.2 %collective-permute-start.24 = (f32[1,2,256]{2,1,0:T(2,128)S(1)}, f32[1,2,256]{2,1,0:T(2,128)S(1)}, u32[]{:S(2)}, u32[]{:S(2)}) collective-permute-start(f32[1,2,256]{2,1,0:T(2,128)S(1)} %fusion.89), channel_id=1, source_target_pairs={{0,4},{4,8},{8,12},{12,16},{16,20},{20,24},{24,28},{1,5},{5,9},{9,... | collective-permute-start | bytes 6152 | tf_op jit(solution)/shard_map/ppermute | solution.py:22
  163.9 4.1 %collective-permute-done.25 = f32[1,2,256]{2,1,0:T(2,128)S(1)} collective-permute-done((f32[1,2,256]{2,1,0:T(2,128)S(1)}, f32[1,2,256]{2,1,0:T(2,128)S(1)}, u32[]{:S(2)}, u32[]{:S(2)}) %collective-permute-start.25) | collective-permute-done | bytes 2080 | tf_op jit(solution)/shard_map/ppermute | solution.py:24
  170.6 2.5 collective-permute-done.27
  174.1 5.6 %reshape.241 = f32[32,2,8,2,8,2]{5,4,3,2,1,0:T(8,128)} reshape(f32[64,256]{1,0:T(8,128)S(1)} %fusion.4) | data formatting | bytes 131072 | tf_op jit(solution)/shard_map/reshape | solution.py:131
  179.7 2.6 reduce_sum.48
  182.5 4.6 %collective-permute-start.31 = (f32[32,8]{0,1:T(8,128)S(1)}, f32[32,8]{0,1:T(8,128)S(1)}, u32[]{:S(2)}, u32[]{:S(2)}) collective-permute-start(f32[32,8]{0,1:T(8,128)S(1)} %get-tuple-element.116), channel_id=1, source_target_pairs={{0,1},{1,2},{2,3},{4,5},{5,6},{6,7},{8,9},{9,10},{10,11},{12,13},{... | collective-permute-start | bytes 3080 | tf_op jit(solution)/shard_map/ppermute | solution.py:22
  188.7 1.3 collective-permute-start.29
  190.0 4.5 %collective-permute-start.28 = (f32[1,64]{0,1:T(8,128)S(1)}, f32[1,64]{0,1:T(8,128)S(1)}, u32[]{:S(2)}, u32[]{:S(2)}) collective-permute-start(f32[1,64]{0,1:T(8,128)S(1)} %constant_dynamic-slice_fusion.2), channel_id=1, source_target_pairs={{0,4},{4,8},{8,12},{12,16},{16,20},{20,24},{24,28},{1,5},{5,9},{9,... | collective-permute-start | bytes 776 | tf_op jit(solution)/shard_map/ppermute | solution.py:22
  194.8 1.4 collective-permute-done.28
  196.5 2.2 collective-permute-start.35
  201.3 5.1 %collective-permute-start.32 = (f32[1,64]{0,1:T(8,128)S(1)}, f32[1,64]{0,1:T(8,128)S(1)}, u32[]{:S(2)}, u32[]{:S(2)}) collective-permute-start(f32[1,64]{0,1:T(8,128)S(1)} %get-tuple-element.105), channel_id=1, source_target_pairs={{0,4},{4,8},{8,12},{12,16},{16,20},{20,24},{24,28},{1,5},{5,9},{9,... | collective-permute-start | bytes 776 | tf_op jit(solution)/shard_map/ppermute | solution.py:22
  206.5 1.4 collective-permute-done.32
  208.3 4.0 %collective-permute-start.39 = (f32[32,8]{0,1:T(8,128)S(1)}, f32[32,8]{0,1:T(8,128)S(1)}, u32[]{:S(2)}, u32[]{:S(2)}) collective-permute-start(f32[32,8]{0,1:T(8,128)S(1)} %get-tuple-element.100), channel_id=1, source_target_pairs={{0,1},{1,2},{2,3},{4,5},{5,6},{6,7},{8,9},{9,10},{10,11},{12,13},{... | collective-permute-start | bytes 3080 | tf_op jit(solution)/shard_map/ppermute | solution.py:22
  213.6 1.5 collective-permute-start.37
  215.1 5.8 %collective-permute-start.36 = (f32[1,64]{0,1:T(8,128)S(1)}, f32[1,64]{0,1:T(8,128)S(1)}, u32[]{:S(2)}, u32[]{:S(2)}) collective-permute-start(f32[1,64]{0,1:T(8,128)S(1)} %get-tuple-element.95), channel_id=1, source_target_pairs={{0,4},{4,8},{8,12},{12,16},{16,20},{20,24},{24,28},{1,5},{5,9},{9,... | collective-permute-start | bytes 776 | tf_op jit(solution)/shard_map/ppermute | solution.py:22
  221.0 1.4 collective-permute-done.36
  222.7 2.4 broadcast_in_dim.422
  225.0 4.0 %reshape.242 = f32[64,256]{1,0:T(8,128)S(1)} reshape(f32[32,2,8,2,8,2]{5,4,3,2,1,0:T(8,128)} %broadcast_in_dim.422) | data formatting | bytes 131072 | tf_op jit(solution)/shard_map/reshape | solution.py:139
  229.2 4.8 %collective-permute-start.40 = (f32[2,2,256]{2,1,0:T(2,128)S(1)}, f32[2,2,256]{2,1,0:T(2,128)S(1)}, u32[]{:S(2)}, u32[]{:S(2)}) collective-permute-start(f32[2,2,256]{2,1,0:T(2,128)S(1)} %get-tuple-element.27), channel_id=1, source_target_pairs={{0,4},{4,8},{8,12},{12,16},{16,20},{20,24},{24,28},{1,5},{5,9},{9,... | collective-permute-start | bytes 12296 | tf_op jit(solution)/shard_map/ppermute | solution.py:22
  235.4 5.4 %collective-permute-done.41 = f32[2,2,256]{2,1,0:T(2,128)S(1)} collective-permute-done((f32[2,2,256]{2,1,0:T(2,128)S(1)}, f32[2,2,256]{2,1,0:T(2,128)S(1)}, u32[]{:S(2)}, u32[]{:S(2)}) %collective-permute-start.41) | collective-permute-done | bytes 4128 | tf_op jit(solution)/shard_map/ppermute | solution.py:24
  240.9 3.1 %collective-permute-start.42 = (f32[2,68,32]{2,1,0:T(8,128)S(1)}, f32[2,68,32]{2,1,0:T(8,128)S(1)}, u32[]{:S(2)}, u32[]{:S(2)}) collective-permute-start(f32[2,68,32]{2,1,0:T(8,128)S(1)} %get-tuple-element.22), channel_id=1, source_target_pairs={{0,1},{1,2},{2,3},{4,5},{5,6},{6,7},{8,9},{9,10},{10,11},{12,13},{... | collective-permute-start | bytes 52232 | tf_op jit(solution)/shard_map/ppermute | solution.py:22
  245.3 5.4 %collective-permute-done.43 = f32[2,68,32]{2,1,0:T(8,128)S(1)} collective-permute-done((f32[2,68,32]{2,1,0:T(8,128)S(1)}, f32[2,68,32]{2,1,0:T(8,128)S(1)}, u32[]{:S(2)}, u32[]{:S(2)}) %collective-permute-start.43) | collective-permute-done | bytes 17440 | tf_op jit(solution)/shard_map/ppermute | solution.py:24
  252.4 44.3 %psum.23 = f32[]{:T(128)} all-reduce(f32[]{:T(128)} %get-tuple-element.7), channel_id=1, replica_groups=mesh['sfc'=8,'grp'=4] {'sfc','grp'}, use_global_device_ids=true, to_apply=%region_7.8 | all-reduce | flops 1 | bytes 8 | tf_op jit(solution)/shard_map/psum | solution.py:191
  (197 shorter events, 39.0 us)
Async XLA Ops:
  2.2 9.1 %collective-permute-start.1 = (f32[1,2,256]{2,1,0:T(2,128)S(1)}, f32[1,2,256]{2,1,0:T(2,128)S(1)}, u32[]{:S(2)}, u32[]{:S(2)}) collective-permute-start(f32[1,2,256]{2,1,0:T(2,128)S(1)} %slice.576), channel_id=1, source_target_pairs={{4,0},{8,4},{12,8},{16,12},{20,16},{24,20},{28,24},{5,1},{9,5},{13... | collective-permute-start | bytes 6152 | tf_op jit(solution)/shard_map/ppermute | solution.py:24
  4.5 6.8 %collective-permute-start = (f32[1,2,256]{2,1,0:T(2,128)S(1)}, f32[1,2,256]{2,1,0:T(2,128)S(1)}, u32[]{:S(2)}, u32[]{:S(2)}) collective-permute-start(f32[1,2,256]{2,1,0:T(2,128)S(1)} %fusion.88), channel_id=1, source_target_pairs={{0,4},{4,8},{8,12},{12,16},{16,20},{20,24},{24,28},{1,5},{5,9},{9,... | collective-permute-start | bytes 6152 | tf_op jit(solution)/shard_map/ppermute | solution.py:22
  11.4 2.8 collective-permute-start.2
  12.7 5.4 %collective-permute-start.3 = (f32[1,68,32]{2,1,0:T(8,128)S(1)}, f32[1,68,32]{2,1,0:T(8,128)S(1)}, u32[]{:S(2)}, u32[]{:S(2)}) collective-permute-start(f32[1,68,32]{2,1,0:T(8,128)S(1)} %get-tuple-element.81), channel_id=1, source_target_pairs={{1,0},{2,1},{3,2},{5,4},{6,5},{7,6},{9,8},{10,9},{11,10},{13,12},{... | collective-permute-start | bytes 26120 | tf_op jit(solution)/shard_map/ppermute | solution.py:24
  27.6 12.4 %collective-permute-start.5 = (f32[1,64]{1,0:T(1,128)S(1)}, f32[1,64]{1,0:T(1,128)S(1)}, u32[]{:S(2)}, u32[]{:S(2)}) collective-permute-start(f32[1,64]{1,0:T(1,128)S(1)} %slice.455), channel_id=1, source_target_pairs={{4,0},{8,4},{12,8},{16,12},{20,16},{24,20},{28,24},{5,1},{9,5},{13... | collective-permute-start | bytes 776 | tf_op jit(solution)/shard_map/ppermute | solution.py:24
  28.9 12.5 %collective-permute-start.7 = (f32[32,8]{0,1:T(8,128)S(1)}, f32[32,8]{0,1:T(8,128)S(1)}, u32[]{:S(2)}, u32[]{:S(2)}) collective-permute-start(f32[32,8]{0,1:T(8,128)S(1)} %get-tuple-element.142), channel_id=1, source_target_pairs={{0,1},{1,2},{2,3},{4,5},{5,6},{6,7},{8,9},{9,10},{10,11},{12,13},{... | collective-permute-start | bytes 3080 | tf_op jit(solution)/shard_map/ppermute | solution.py:22
  33.5 7.9 %collective-permute-start.6 = (f32[32,8]{0,1:T(8,128)S(1)}, f32[32,8]{0,1:T(8,128)S(1)}, u32[]{:S(2)}, u32[]{:S(2)}) collective-permute-start(f32[32,8]{0,1:T(8,128)S(1)} %get-tuple-element.143), channel_id=1, source_target_pairs={{1,0},{2,1},{3,2},{5,4},{6,5},{7,6},{9,8},{10,9},{11,10},{13,12},{... | collective-permute-start | bytes 3080 | tf_op jit(solution)/shard_map/ppermute | solution.py:24
  34.9 6.5 %collective-permute-start.4 = (f32[1,64]{0,1:T(8,128)S(1)}, f32[1,64]{0,1:T(8,128)S(1)}, u32[]{:S(2)}, u32[]{:S(2)}) collective-permute-start(f32[1,64]{0,1:T(8,128)S(1)} %constant_dynamic-slice_fusion.7), channel_id=1, source_target_pairs={{0,4},{4,8},{8,12},{12,16},{16,20},{20,24},{24,28},{1,5},{5,9},{9,... | collective-permute-start | bytes 776 | tf_op jit(solution)/shard_map/ppermute | solution.py:22
  41.7 12.2 %collective-permute-start.11 = (f32[32,8]{0,1:T(8,128)S(1)}, f32[32,8]{0,1:T(8,128)S(1)}, u32[]{:S(2)}, u32[]{:S(2)}) collective-permute-start(f32[32,8]{0,1:T(8,128)S(1)} %get-tuple-element.136), channel_id=1, source_target_pairs={{0,1},{1,2},{2,3},{4,5},{5,6},{6,7},{8,9},{9,10},{10,11},{12,13},{... | collective-permute-start | bytes 3080 | tf_op jit(solution)/shard_map/ppermute | solution.py:22
  44.0 9.9 %collective-permute-start.10 = (f32[32,8]{0,1:T(8,128)S(1)}, f32[32,8]{0,1:T(8,128)S(1)}, u32[]{:S(2)}, u32[]{:S(2)}) collective-permute-start(f32[32,8]{0,1:T(8,128)S(1)} %get-tuple-element.137), channel_id=1, source_target_pairs={{1,0},{2,1},{3,2},{5,4},{6,5},{7,6},{9,8},{10,9},{11,10},{13,12},{... | collective-permute-start | bytes 3080 | tf_op jit(solution)/shard_map/ppermute | solution.py:24
  45.3 7.0 %collective-permute-start.9 = (f32[1,64]{0,1:T(8,128)S(1)}, f32[1,64]{0,1:T(8,128)S(1)}, u32[]{:S(2)}, u32[]{:S(2)}) collective-permute-start(f32[1,64]{0,1:T(8,128)S(1)} %get-tuple-element.130), channel_id=1, source_target_pairs={{4,0},{8,4},{12,8},{16,12},{20,16},{24,20},{28,24},{5,1},{9,5},{13... | collective-permute-start | bytes 776 | tf_op jit(solution)/shard_map/ppermute | solution.py:24
  46.6 7.3 %collective-permute-start.8 = (f32[1,64]{0,1:T(8,128)S(1)}, f32[1,64]{0,1:T(8,128)S(1)}, u32[]{:S(2)}, u32[]{:S(2)}) collective-permute-start(f32[1,64]{0,1:T(8,128)S(1)} %get-tuple-element.131), channel_id=1, source_target_pairs={{0,4},{4,8},{8,12},{12,16},{16,20},{20,24},{24,28},{1,5},{5,9},{9,... | collective-permute-start | bytes 776 | tf_op jit(solution)/shard_map/ppermute | solution.py:22
  54.2 13.6 %collective-permute-start.15 = (f32[32,8]{0,1:T(8,128)S(1)}, f32[32,8]{0,1:T(8,128)S(1)}, u32[]{:S(2)}, u32[]{:S(2)}) collective-permute-start(f32[32,8]{0,1:T(8,128)S(1)} %get-tuple-element.126), channel_id=1, source_target_pairs={{0,1},{1,2},{2,3},{4,5},{5,6},{6,7},{8,9},{9,10},{10,11},{12,13},{... | collective-permute-start | bytes 3080 | tf_op jit(solution)/shard_map/ppermute | solution.py:22
  57.9 9.9 %collective-permute-start.14 = (f32[32,8]{0,1:T(8,128)S(1)}, f32[32,8]{0,1:T(8,128)S(1)}, u32[]{:S(2)}, u32[]{:S(2)}) collective-permute-start(f32[32,8]{0,1:T(8,128)S(1)} %get-tuple-element.127), channel_id=1, source_target_pairs={{1,0},{2,1},{3,2},{5,4},{6,5},{7,6},{9,8},{10,9},{11,10},{13,12},{... | collective-permute-start | bytes 3080 | tf_op jit(solution)/shard_map/ppermute | solution.py:24
  59.2 7.1 %collective-permute-start.13 = (f32[1,64]{0,1:T(8,128)S(1)}, f32[1,64]{0,1:T(8,128)S(1)}, u32[]{:S(2)}, u32[]{:S(2)}) collective-permute-start(f32[1,64]{0,1:T(8,128)S(1)} %get-tuple-element.120), channel_id=1, source_target_pairs={{4,0},{8,4},{12,8},{16,12},{20,16},{24,20},{28,24},{5,1},{9,5},{13... | collective-permute-start | bytes 776 | tf_op jit(solution)/shard_map/ppermute | solution.py:24
  60.5 7.3 %collective-permute-start.12 = (f32[1,64]{0,1:T(8,128)S(1)}, f32[1,64]{0,1:T(8,128)S(1)}, u32[]{:S(2)}, u32[]{:S(2)}) collective-permute-start(f32[1,64]{0,1:T(8,128)S(1)} %get-tuple-element.121), channel_id=1, source_target_pairs={{0,4},{4,8},{8,12},{12,16},{16,20},{20,24},{24,28},{1,5},{5,9},{9,... | collective-permute-start | bytes 776 | tf_op jit(solution)/shard_map/ppermute | solution.py:22
  74.5 36.5 %copy-start.1 = (f32[4,16,256]{2,1,0:T(8,128)S(1)}, f32[4,16,256]{2,1,0:T(8,128)}, u32[]{:S(2)}) copy-start(f32[4,16,256]{2,1,0:T(8,128)} %param.2) | copy-start | bytes 196612
  74.6 6.2 %collective-permute-start.16 = (f32[2,2,256]{2,1,0:T(2,128)S(1)}, f32[2,2,256]{2,1,0:T(2,128)S(1)}, u32[]{:S(2)}, u32[]{:S(2)}) collective-permute-start(f32[2,2,256]{2,1,0:T(2,128)S(1)} %get-tuple-element.31), channel_id=1, source_target_pairs={{0,4},{4,8},{8,12},{12,16},{16,20},{20,24},{24,28},{1,5},{5,9},{9,... | collective-permute-start | bytes 12296 | tf_op jit(solution)/shard_map/ppermute | solution.py:22
  79.5 6.8 %collective-permute-start.17 = (f32[2,2,256]{2,1,0:T(2,128)S(1)}, f32[2,2,256]{2,1,0:T(2,128)S(1)}, u32[]{:S(2)}, u32[]{:S(2)}) collective-permute-start(f32[2,2,256]{2,1,0:T(2,128)S(1)} %get-tuple-element.30), channel_id=1, source_target_pairs={{4,0},{8,4},{12,8},{16,12},{20,16},{24,20},{28,24},{5,1},{9,5},{13... | collective-permute-start | bytes 12296 | tf_op jit(solution)/shard_map/ppermute | solution.py:24
  86.3 4.4 %collective-permute-start.18 = (f32[2,68,32]{2,1,0:T(8,128)S(1)}, f32[2,68,32]{2,1,0:T(8,128)S(1)}, u32[]{:S(2)}, u32[]{:S(2)}) collective-permute-start(f32[2,68,32]{2,1,0:T(8,128)S(1)} %get-tuple-element.24), channel_id=1, source_target_pairs={{0,1},{1,2},{2,3},{4,5},{5,6},{6,7},{8,9},{9,10},{10,11},{12,13},{... | collective-permute-start | bytes 52232 | tf_op jit(solution)/shard_map/ppermute | solution.py:22
  89.4 6.7 %collective-permute-start.19 = (f32[2,68,32]{2,1,0:T(8,128)S(1)}, f32[2,68,32]{2,1,0:T(8,128)S(1)}, u32[]{:S(2)}, u32[]{:S(2)}) collective-permute-start(f32[2,68,32]{2,1,0:T(8,128)S(1)} %get-tuple-element.25), channel_id=1, source_target_pairs={{1,0},{2,1},{3,2},{5,4},{6,5},{7,6},{9,8},{10,9},{11,10},{13,12},{... | collective-permute-start | bytes 52232 | tf_op jit(solution)/shard_map/ppermute | solution.py:24
  97.4 12.7 %collective-permute-start.20 = (f32[1,256]{1,0:T(1,128)S(1)}, f32[1,256]{1,0:T(1,128)S(1)}, u32[]{:S(2)}, u32[]{:S(2)}) collective-permute-start(f32[1,256]{1,0:T(1,128)S(1)} %get-tuple-element.84), channel_id=1, source_target_pairs={{0,4},{4,8},{8,12},{12,16},{16,20},{20,24},{24,28},{1,5},{5,9},{9,... | collective-permute-start | bytes 3080 | tf_op jit(solution)/shard_map/ppermute | solution.py:22
  102.3 7.9 %collective-permute-start.21 = (f32[1,256]{1,0:T(1,128)S(1)}, f32[1,256]{1,0:T(1,128)S(1)}, u32[]{:S(2)}, u32[]{:S(2)}) collective-permute-start(f32[1,256]{1,0:T(1,128)S(1)} %get-tuple-element.85), channel_id=1, source_target_pairs={{4,0},{8,4},{12,8},{16,12},{20,16},{24,20},{28,24},{5,1},{9,5},{13... | collective-permute-start | bytes 3080 | tf_op jit(solution)/shard_map/ppermute | solution.py:24
  103.6 6.6 %collective-permute-start.22 = (f32[64,16]{1,0:T(8,128)S(1)}, f32[64,16]{1,0:T(8,128)S(1)}, u32[]{:S(2)}, u32[]{:S(2)}) collective-permute-start(f32[64,16]{1,0:T(8,128)S(1)} %get-tuple-element.90), channel_id=1, source_target_pairs={{1,0},{2,1},{3,2},{5,4},{6,5},{7,6},{9,8},{10,9},{11,10},{13,12},{... | collective-permute-start | bytes 12296 | tf_op jit(solution)/shard_map/ppermute | solution.py:24
  104.9 6.1 %collective-permute-start.23 = (f32[64,16]{1,0:T(8,128)S(1)}, f32[64,16]{1,0:T(8,128)S(1)}, u32[]{:S(2)}, u32[]{:S(2)}) collective-permute-start(f32[64,16]{1,0:T(8,128)S(1)} %get-tuple-element.91), channel_id=1, source_target_pairs={{0,1},{1,2},{2,3},{4,5},{5,6},{6,7},{8,9},{9,10},{10,11},{12,13},{... | collective-permute-start | bytes 12296 | tf_op jit(solution)/shard_map/ppermute | solution.py:22
  158.3 77.1 %copy-start = (f32[64,256]{1,0:T(8,128)}, f32[64,256]{1,0:T(8,128)S(1)}, u32[]{:S(2)}) copy-start(f32[64,256]{1,0:T(8,128)S(1)} %multiply_subtract_fusion.1) | copy-start | bytes 196612
  158.3 5.5 %collective-permute-start.24 = (f32[1,2,256]{2,1,0:T(2,128)S(1)}, f32[1,2,256]{2,1,0:T(2,128)S(1)}, u32[]{:S(2)}, u32[]{:S(2)}) collective-permute-start(f32[1,2,256]{2,1,0:T(2,128)S(1)} %fusion.89), channel_id=1, source_target_pairs={{0,4},{4,8},{8,12},{12,16},{16,20},{20,24},{24,28},{1,5},{5,9},{9,... | collective-permute-start | bytes 6152 | tf_op jit(solution)/shard_map/ppermute | solution.py:22
  162.5 5.5 %collective-permute-start.25 = (f32[1,2,256]{2,1,0:T(2,128)S(1)}, f32[1,2,256]{2,1,0:T(2,128)S(1)}, u32[]{:S(2)}, u32[]{:S(2)}) collective-permute-start(f32[1,2,256]{2,1,0:T(2,128)S(1)} %slice.654), channel_id=1, source_target_pairs={{4,0},{8,4},{12,8},{16,12},{20,16},{24,20},{28,24},{5,1},{9,5},{13... | collective-permute-start | bytes 6152 | tf_op jit(solution)/shard_map/ppermute | solution.py:24
  168.0 2.6 collective-permute-start.26
  169.3 3.8 %collective-permute-start.27 = (f32[1,68,32]{2,1,0:T(8,128)S(1)}, f32[1,68,32]{2,1,0:T(8,128)S(1)}, u32[]{:S(2)}, u32[]{:S(2)}) collective-permute-start(f32[1,68,32]{2,1,0:T(8,128)S(1)} %get-tuple-element.79), channel_id=1, source_target_pairs={{1,0},{2,1},{3,2},{5,4},{6,5},{7,6},{9,8},{10,9},{11,10},{13,12},{... | collective-permute-start | bytes 26120 | tf_op jit(solution)/shard_map/ppermute | solution.py:24
  182.5 13.6 %collective-permute-start.31 = (f32[32,8]{0,1:T(8,128)S(1)}, f32[32,8]{0,1:T(8,128)S(1)}, u32[]{:S(2)}, u32[]{:S(2)}) collective-permute-start(f32[32,8]{0,1:T(8,128)S(1)} %get-tuple-element.116), channel_id=1, source_target_pairs={{0,1},{1,2},{2,3},{4,5},{5,6},{6,7},{8,9},{9,10},{10,11},{12,13},{... | collective-permute-start | bytes 3080 | tf_op jit(solution)/shard_map/ppermute | solution.py:22
  187.1 9.1 %collective-permute-start.30 = (f32[32,8]{0,1:T(8,128)S(1)}, f32[32,8]{0,1:T(8,128)S(1)}, u32[]{:S(2)}, u32[]{:S(2)}) collective-permute-start(f32[32,8]{0,1:T(8,128)S(1)} %get-tuple-element.117), channel_id=1, source_target_pairs={{1,0},{2,1},{3,2},{5,4},{6,5},{7,6},{9,8},{10,9},{11,10},{13,12},{... | collective-permute-start | bytes 3080 | tf_op jit(solution)/shard_map/ppermute | solution.py:24
  188.7 6.1 %collective-permute-start.29 = (f32[1,64]{1,0:T(1,128)S(1)}, f32[1,64]{1,0:T(1,128)S(1)}, u32[]{:S(2)}, u32[]{:S(2)}) collective-permute-start(f32[1,64]{1,0:T(1,128)S(1)} %slice.531), channel_id=1, source_target_pairs={{4,0},{8,4},{12,8},{16,12},{20,16},{24,20},{28,24},{5,1},{9,5},{13... | collective-permute-start | bytes 776 | tf_op jit(solution)/shard_map/ppermute | solution.py:24
  190.0 6.2 %collective-permute-start.28 = (f32[1,64]{0,1:T(8,128)S(1)}, f32[1,64]{0,1:T(8,128)S(1)}, u32[]{:S(2)}, u32[]{:S(2)}) collective-permute-start(f32[1,64]{0,1:T(8,128)S(1)} %constant_dynamic-slice_fusion.2), channel_id=1, source_target_pairs={{0,4},{4,8},{8,12},{12,16},{16,20},{20,24},{24,28},{1,5},{5,9},{9,... | collective-permute-start | bytes 776 | tf_op jit(solution)/shard_map/ppermute | solution.py:22
  196.5 11.5 %collective-permute-start.35 = (f32[32,8]{0,1:T(8,128)S(1)}, f32[32,8]{0,1:T(8,128)S(1)}, u32[]{:S(2)}, u32[]{:S(2)}) collective-permute-start(f32[32,8]{0,1:T(8,128)S(1)} %get-tuple-element.110), channel_id=1, source_target_pairs={{0,1},{1,2},{2,3},{4,5},{5,6},{6,7},{8,9},{9,10},{10,11},{12,13},{... | collective-permute-start | bytes 3080 | tf_op jit(solution)/shard_map/ppermute | solution.py:22
  198.7 9.3 %collective-permute-start.34 = (f32[32,8]{0,1:T(8,128)S(1)}, f32[32,8]{0,1:T(8,128)S(1)}, u32[]{:S(2)}, u32[]{:S(2)}) collective-permute-start(f32[32,8]{0,1:T(8,128)S(1)} %get-tuple-element.111), channel_id=1, source_target_pairs={{1,0},{2,1},{3,2},{5,4},{6,5},{7,6},{9,8},{10,9},{11,10},{13,12},{... | collective-permute-start | bytes 3080 | tf_op jit(solution)/shard_map/ppermute | solution.py:24
  200.0 6.4 %collective-permute-start.33 = (f32[1,64]{0,1:T(8,128)S(1)}, f32[1,64]{0,1:T(8,128)S(1)}, u32[]{:S(2)}, u32[]{:S(2)}) collective-permute-start(f32[1,64]{0,1:T(8,128)S(1)} %get-tuple-element.104), channel_id=1, source_target_pairs={{4,0},{8,4},{12,8},{16,12},{20,16},{24,20},{28,24},{5,1},{9,5},{13... | collective-permute-start | bytes 776 | tf_op jit(solution)/shard_map/ppermute | solution.py:24
  201.3 6.7 %collective-permute-start.32 = (f32[1,64]{0,1:T(8,128)S(1)}, f32[1,64]{0,1:T(8,128)S(1)}, u32[]{:S(2)}, u32[]{:S(2)}) collective-permute-start(f32[1,64]{0,1:T(8,128)S(1)} %get-tuple-element.105), channel_id=1, source_target_pairs={{0,4},{4,8},{8,12},{12,16},{16,20},{20,24},{24,28},{1,5},{5,9},{9,... | collective-permute-start | bytes 776 | tf_op jit(solution)/shard_map/ppermute | solution.py:22
  208.3 14.1 %collective-permute-start.39 = (f32[32,8]{0,1:T(8,128)S(1)}, f32[32,8]{0,1:T(8,128)S(1)}, u32[]{:S(2)}, u32[]{:S(2)}) collective-permute-start(f32[32,8]{0,1:T(8,128)S(1)} %get-tuple-element.100), channel_id=1, source_target_pairs={{0,1},{1,2},{2,3},{4,5},{5,6},{6,7},{8,9},{9,10},{10,11},{12,13},{... | collective-permute-start | bytes 3080 | tf_op jit(solution)/shard_map/ppermute | solution.py:22
  212.3 10.1 %collective-permute-start.38 = (f32[32,8]{0,1:T(8,128)S(1)}, f32[32,8]{0,1:T(8,128)S(1)}, u32[]{:S(2)}, u32[]{:S(2)}) collective-permute-start(f32[32,8]{0,1:T(8,128)S(1)} %get-tuple-element.101), channel_id=1, source_target_pairs={{1,0},{2,1},{3,2},{5,4},{6,5},{7,6},{9,8},{10,9},{11,10},{13,12},{... | collective-permute-start | bytes 3080 | tf_op jit(solution)/shard_map/ppermute | solution.py:24
  213.6 7.3 %collective-permute-start.37 = (f32[1,64]{0,1:T(8,128)S(1)}, f32[1,64]{0,1:T(8,128)S(1)}, u32[]{:S(2)}, u32[]{:S(2)}) collective-permute-start(f32[1,64]{0,1:T(8,128)S(1)} %get-tuple-element.94), channel_id=1, source_target_pairs={{4,0},{8,4},{12,8},{16,12},{20,16},{24,20},{28,24},{5,1},{9,5},{13... | collective-permute-start | bytes 776 | tf_op jit(solution)/shard_map/ppermute | solution.py:24
  215.1 7.3 %collective-permute-start.36 = (f32[1,64]{0,1:T(8,128)S(1)}, f32[1,64]{0,1:T(8,128)S(1)}, u32[]{:S(2)}, u32[]{:S(2)}) collective-permute-start(f32[1,64]{0,1:T(8,128)S(1)} %get-tuple-element.95), channel_id=1, source_target_pairs={{0,4},{4,8},{8,12},{12,16},{16,20},{20,24},{24,28},{1,5},{5,9},{9,... | collective-permute-start | bytes 776 | tf_op jit(solution)/shard_map/ppermute | solution.py:22
  229.2 6.1 %collective-permute-start.40 = (f32[2,2,256]{2,1,0:T(2,128)S(1)}, f32[2,2,256]{2,1,0:T(2,128)S(1)}, u32[]{:S(2)}, u32[]{:S(2)}) collective-permute-start(f32[2,2,256]{2,1,0:T(2,128)S(1)} %get-tuple-element.27), channel_id=1, source_target_pairs={{0,4},{4,8},{8,12},{12,16},{16,20},{20,24},{24,28},{1,5},{5,9},{9,... | collective-permute-start | bytes 12296 | tf_op jit(solution)/shard_map/ppermute | solution.py:22
  234.0 6.8 %collective-permute-start.41 = (f32[2,2,256]{2,1,0:T(2,128)S(1)}, f32[2,2,256]{2,1,0:T(2,128)S(1)}, u32[]{:S(2)}, u32[]{:S(2)}) collective-permute-start(f32[2,2,256]{2,1,0:T(2,128)S(1)} %get-tuple-element.26), channel_id=1, source_target_pairs={{4,0},{8,4},{12,8},{16,12},{20,16},{24,20},{28,24},{5,1},{9,5},{13... | collective-permute-start | bytes 12296 | tf_op jit(solution)/shard_map/ppermute | solution.py:24
  240.9 4.4 %collective-permute-start.42 = (f32[2,68,32]{2,1,0:T(8,128)S(1)}, f32[2,68,32]{2,1,0:T(8,128)S(1)}, u32[]{:S(2)}, u32[]{:S(2)}) collective-permute-start(f32[2,68,32]{2,1,0:T(8,128)S(1)} %get-tuple-element.22), channel_id=1, source_target_pairs={{0,1},{1,2},{2,3},{4,5},{5,6},{6,7},{8,9},{9,10},{10,11},{12,13},{... | collective-permute-start | bytes 52232 | tf_op jit(solution)/shard_map/ppermute | solution.py:22
  244.0 6.7 %collective-permute-start.43 = (f32[2,68,32]{2,1,0:T(8,128)S(1)}, f32[2,68,32]{2,1,0:T(8,128)S(1)}, u32[]{:S(2)}, u32[]{:S(2)}) collective-permute-start(f32[2,68,32]{2,1,0:T(8,128)S(1)} %get-tuple-element.23), channel_id=1, source_target_pairs={{1,0},{2,1},{3,2},{5,4},{6,5},{7,6},{9,8},{10,9},{11,10},{13,12},{... | collective-permute-start | bytes 52232 | tf_op jit(solution)/shard_map/ppermute | solution.py:24
where the time goes:
time: 300 us; the launch traced here: 299 us
  starting transfers between devices  120 us (40%)
  blocking collectives  89.4 us (30%)
  waiting for transfers between devices  42.4 us (14%)
  local copies, waits for them, and re-layouts  28.7 us (10%)
  other arithmetic  13.1 us (4%)
  between operations  5.23 us (2%)
    ppermute x22, starting transfers between devices, padded_2(): lax.ppermute(tail, axis, [(i, (i + 1) % count) for i in range(ends)])  91.2 us
    psum x1, blocking collectives, shards(): rz_value = lax.psum(jnp.sum(first_rhs * first_z), ('sfc', 'grp'))  45.1 us
    psum x1, blocking collectives, shards(): cross = lax.psum(jnp.sum(next_z * image), ('sfc', 'grp'))  44.3 us
    ppermute x22, waiting for transfers between devices, padded_2(): lax.ppermute(head, axis, [((i + 1) % count, i) for i in range(ends)])  32.1 us
    ppermute x22, starting transfers between devices, padded_2(): lax.ppermute(head, axis, [((i + 1) % count, i) for i in range(ends)])  28.6 us
    reshape x2, local copies, waits for them, and re-layouts, restrict(): blocks = field.reshape(planes // 2, 2, half, 2, half, 2)  11.2 us
    ppermute x22, waiting for transfers between devices, padded_2(): lax.ppermute(tail, axis, [(i, (i + 1) % count) for i in range(ends)])  10.3 us
    reshape x2, local copies, waits for them, and re-layouts, prolong(): return blocks.reshape(planes * 2, 4 * half * half)  8.07 us
  transfers between devices with their start and end apart: 44, of which 15 were waited for; matrix products, arithmetic and copies ran while one was open for 1% of the time, Pallas kernels for 0%

commit v1 on v0

v1 whole, which is shorter than its diff:
```python
import functools

import jax
import jax.numpy as jnp
from jax import lax
from jax.experimental import pallas as pl
from jax.experimental.pallas import tpu as pltpu
from jax.sharding import PartitionSpec as P

PRE_SWEEPS = 2
POST_SWEEPS = 2
COARSE_SWEEPS = 4
OMEGA = 2.0 / 3.0
LANES = 128
ROWS = 8


def halo_depth():
    def down_even(plane):
        return plane + plane % 2

    def cycle(reach):
        return down_even(reach + POST_SWEEPS) + 2 * (COARSE_SWEEPS - 1) + PRE_SWEEPS

    return -(-cycle(cycle(0) + 1) // ROWS) * ROWS


def shift_lanes(value, amount):
    return pltpu.roll(value, amount % LANES, 1)


def neighbours(value, reach, edge):
    rows = value.shape[0]
    lane = lax.broadcasted_iota(jnp.int32, value.shape, 1)
    row = lax.broadcasted_iota(jnp.int32, value.shape, 0)
    column = lane % edge
    hop = reach * edge
    up = jnp.where(column < edge - reach, shift_lanes(value, -reach), 0.0)
    down = jnp.where(column >= reach, shift_lanes(value, reach), 0.0)
    ahead = shift_lanes(value, -hop)
    over = jnp.where(row == rows - 1, 0.0, pltpu.roll(ahead, rows - 1, 0))
    north = jnp.where(lane < LANES - hop, ahead, over)
    behind = shift_lanes(value, hop)
    under = jnp.where(row == 0, 0.0, pltpu.roll(behind, 1, 0))
    south = jnp.where(lane >= hop, behind, under)
    return (up + down) + (north + south)


def block_sum(value, edge):
    lane = lax.broadcasted_iota(jnp.int32, value.shape, 1)
    even_z = lane % 2 == 0
    value = value + jnp.where(even_z, shift_lanes(value, -1), shift_lanes(value, 1))
    even_y = (lane // edge) % 2 == 0
    return value + jnp.where(even_y, shift_lanes(value, -edge), shift_lanes(value, edge))


def cycles_kernel(
    depth, edge, tile, scalars, cells, z_out, image_out, again_out, sums_out,
    r_ref, z_ref, t_ref, image_ref, c_ref, e_ref, f_ref,
):
    groups, padded, width = cells.shape
    planes = padded - 2 * depth
    parts = width // LANES
    count, above, under, group = scalars[0], scalars[1], scalars[2], scalars[3]
    first = (depth - above) // ROWS
    live_end = depth + count * edge
    last = (live_end + under) // ROWS
    own_first, own_last = depth // ROWS, live_end // ROWS
    step = OMEGA / 6.0
    coarse_step = OMEGA / 1.5
    half_rows = ROWS // 2

    def at(plane):
        return pl.ds(pl.multiple_of((plane + 1) * tile, ROWS), tile)

    for ref in (r_ref, z_ref, t_ref, image_ref, c_ref, e_ref, f_ref):
        ref[...] = jnp.zeros(ref.shape, jnp.float32)

    for block in range(padded // ROWS):
        low = block * ROWS
        target = low if low < depth + planes else live_end + (low - depth - planes)
        for part in range(groups * parts):
            rows = pl.ds((target + 1) * tile + part, ROWS, stride=tile)
            lanes = slice(part % parts * LANES, (part % parts + 1) * LANES)
            r_ref[rows, :] = cells[part // parts, low : low + ROWS, lanes]

    def sweep(begin, end, size, reach, source, emit):
        def body(block, carry):
            base = block * size
            window = [source[at(base + k), :] for k in range(-1, size + 1)]
            applied = []
            for k in range(size):
                middle = window[k + 1]
                around = neighbours(middle, reach, edge) + (window[k] + window[k + 2])
                applied.append(6.0 * middle - around)
            emit(base, window[1:-1], applied)
            return carry

        lax.fori_loop(begin, end, body, 0)

    def cycle(rhs):
        def first_sweep(base, middle, applied):
            for k in range(ROWS):
                z_ref[at(base + k), :] = step * (2.0 * middle[k] - step * applied[k])

        sweep(first, last, ROWS, 1, rhs, first_sweep)

        def coarsen(base, middle, applied):
            for k in range(half_rows):
                pair = (rhs[at(base + 2 * k), :] - applied[2 * k]) + (
                    rhs[at(base + 2 * k + 1), :] - applied[2 * k + 1]
                )
                c_ref[at(base // 2 + k), :] = 0.125 * block_sum(pair, edge)

        sweep(first, last, ROWS, 1, z_ref, coarsen)

        def coarse_start(base, middle, applied):
            for k in range(half_rows):
                e_ref[at(base + k), :] = coarse_step * (
                    2.0 * middle[k] - (0.25 * coarse_step) * applied[k]
                )

        sweep(first, last, half_rows, 2, c_ref, coarse_start)
        held, spare = e_ref, f_ref
        for index in range(COARSE_SWEEPS - 2):
            final = index == COARSE_SWEEPS - 3

            def coarse_next(base, middle, applied, spare=spare, final=final):
                for k in range(half_rows):
                    value = middle[k] + coarse_step * (
                        c_ref[at(base + k), :] - 0.25 * applied[k]
                    )
                    if final:
                        for fine in (2 * (base + k), 2 * (base + k) + 1):
                            z_ref[at(fine), :] = z_ref[at(fine), :] + value
                    else:
                        spare[at(base + k), :] = value

            sweep(first, last, half_rows, 2, held, coarse_next)
            held, spare = spare, held

        here, there = z_ref, t_ref
        for index in range(POST_SWEEPS):

            def smooth(base, middle, applied, there=there):
                for k in range(ROWS):
                    there[at(base + k), :] = middle[k] + step * (
                        rhs[at(base + k), :] - applied[k]
                    )

            sweep(first, last, ROWS, 1, here, smooth)
            here, there = there, here
        return here

    def store(ref, out):
        for block in range(planes // ROWS):
            for part in range(parts):
                begin = (depth + block * ROWS + 1) * tile + group * parts + part
                value = ref[pl.ds(begin, ROWS, stride=tile), :]
                lanes = slice(part * LANES, (part + 1) * LANES)
                rows = slice(block * ROWS, (block + 1) * ROWS)
                out[rows, lanes] = jnp.where(block * ROWS < count * edge, value, 0.0)

    zero = jnp.zeros((tile, LANES), jnp.float32)
    result = cycle(r_ref)
    store(result, z_out)

    def to_image(base, middle, applied):
        for k in range(ROWS):
            image_ref[at(base + k), :] = applied[k]

    sweep(first, last, ROWS, 1, result, to_image)
    store(image_ref, image_out)

    def first_sums(block, carry):
        rz, curv = carry
        for k in range(ROWS):
            rows = at(block * ROWS + k)
            rz = rz + r_ref[rows, :] * result[rows, :]
            curv = curv + result[rows, :] * image_ref[rows, :]
        return rz, curv

    rz, curv = lax.fori_loop(own_first, own_last, first_sums, (zero, zero))
    again = cycle(image_ref)
    store(again, again_out)

    def last_sum(block, mixed):
        for k in range(ROWS):
            rows = at(block * ROWS + k)
            mixed = mixed + again[rows, :] * image_ref[rows, :]
        return mixed

    mixed = lax.fori_loop(own_first, own_last, last_sum, zero)
    row = lax.broadcasted_iota(jnp.int32, (ROWS, LANES), 0)
    packed = jnp.zeros((ROWS, LANES), jnp.float32)
    for index, value in enumerate((rz, curv, mixed)):
        total = jnp.sum(value, axis=0, keepdims=True)
        packed = jnp.where(row == index, total, packed)
    for peer in range(sums_out.shape[0] // ROWS):
        sums_out[peer * ROWS : (peer + 1) * ROWS, :] = packed


def finish_kernel(sums, r_ref, z_ref, image_ref, again_ref, solution, residual, direction):
    peers = sums.shape[0] // ROWS
    total = sums[:ROWS, :]
    for peer in range(1, peers):
        total = total + sums[peer * ROWS : (peer + 1) * ROWS, :]
    total = jnp.sum(total, axis=1, keepdims=True)
    rz, curv, mixed = total[0:1], total[1:2], total[2:3]
    alpha = rz / curv
    share = mixed / curv
    z = z_ref[...]
    solution[...] = alpha * z
    residual[...] = r_ref[...] - alpha * image_ref[...]
    direction[...] = alpha * (share * z - again_ref[...])


def send(value, hop):
    count = lax.axis_size("sfc")
    pairs = [(i, (i + hop) % count) for i in range(count)]
    return lax.ppermute(value, "sfc", pairs)


def shards(source, layer_counts):
    count = layer_counts[0]
    slots, edge, width = source.shape
    planes = slots * edge
    depth = halo_depth()
    far = depth - edge
    groups, peers = lax.axis_size("grp"), lax.axis_size("sfc")
    tile = groups * width // LANES
    plane = lax.broadcasted_iota(jnp.int32, (planes, 1), 0)
    own = jnp.where(plane < count * edge, source.reshape(planes, width), 0.0)
    mark = jnp.full((ROWS, width), count.astype(jnp.float32))
    padded = jnp.concatenate([jnp.zeros((far, width), jnp.float32), own], axis=0)
    tail = lax.dynamic_slice_in_dim(padded, count * edge - edge, depth, 0)
    far_tail = lax.dynamic_slice_in_dim(own, count * edge - far, far, 0)
    from_back = send(jnp.concatenate([tail, mark], axis=0), 1)
    from_front = send(jnp.concatenate([own[:depth], mark], axis=0), -1)
    from_far_back = send(far_tail, 2)
    from_far_front = send(own[:far], -2)
    back_count, front_count = from_back[depth, 0], from_front[depth, 0]
    index = lax.axis_index("sfc")
    back_thin, front_thin = back_count < 1.5, front_count < 1.5
    back, front = index > 0, index < peers - 1
    far_back = jnp.where(index > 1, from_far_back, 0.0)
    far_front = jnp.where(index < peers - 2, from_far_front, 0.0)
    cells = jnp.concatenate(
        [
            jnp.where(back, jnp.where(back_thin, far_back, from_back[:far]), 0.0),
            jnp.where(back, from_back[far:depth], 0.0),
            own,
            jnp.where(front, from_front[:edge], 0.0),
            jnp.where(front, jnp.where(front_thin, far_front, from_front[edge:depth]), 0.0),
        ],
        axis=0,
    )
    above = jnp.where((index == 1) & back_thin, edge, depth)
    above = jnp.where(index == 0, 0, above)
    under = jnp.where((index == peers - 2) & front_thin, edge, depth)
    under = jnp.where(index == peers - 1, 0, under)
    scalars = jnp.stack([count, above, under, lax.axis_index("grp")]).astype(jnp.int32)
    gathered = lax.all_gather(cells, "grp", axis=0, tiled=False)
    fine = pltpu.VMEM(((planes + 2 * depth + 2) * tile, LANES), jnp.float32)
    coarse = pltpu.VMEM(((planes // 2 + depth + 2) * tile, LANES), jnp.float32)
    block = jax.ShapeDtypeStruct((planes, width), jnp.float32)
    vmem = pl.BlockSpec(memory_space=pltpu.VMEM)
    z, image, again, sums = pl.pallas_call(
        functools.partial(cycles_kernel, depth, edge, tile),
        out_shape=[block, block, block, jax.ShapeDtypeStruct((peers * ROWS, LANES), jnp.float32)],
        in_specs=[pl.BlockSpec(memory_space=pltpu.SMEM), vmem],
        out_specs=[vmem] * 4,
        scratch_shapes=[fine, fine, fine, fine, coarse, coarse, coarse],
    )(scalars, gathered)
    sums = lax.all_to_all(sums, "sfc", 0, 0, tiled=True)
    outs = pl.pallas_call(
        finish_kernel,
        out_shape=[block] * 3,
        in_specs=[vmem] * 5,
        out_specs=[vmem] * 3,
    )(sums, own, z, image, again)
    return tuple(out.reshape(slots, edge, width) for out in outs)


def solution(mesh):
    return jax.shard_map(
        shards,
        mesh=mesh,
        in_specs=(P("sfc", None, "grp"), P("sfc")),
        out_specs=(P("sfc", None, "grp"), P("sfc", None, "grp"), P("sfc", None, "grp")),
        check_vma=False,
    )
```

time: 300 us -> 62.2 us (0.21)
  starting transfers between devices: 120 us -> 10.5 us
  blocking collectives: 89.4 us -> 24.4 us
  waiting for transfers between devices: 42.4 us -> 1.25 us
  local copies, waits for them, and re-layouts: 28.7 us -> 1.06 us
  Pallas kernels: 0 us -> 20.2 us
  other arithmetic: 13.1 us -> 1.66 us
    ppermute x44 -> x4, starting transfers between devices: 120 us -> 10.5 us  [send(): return lax.ppermute(value, 'sfc', pairs)]
    psum x2 -> x0, blocking collectives: 89.4 us -> none  [the longest x1 45.1 us: shards(): rz_value = lax.psum(jnp.sum(first_rhs * first_z), ('sfc', 'grp'))]
    ppermute x44 -> x4, waiting for transfers between devices: 42.4 us -> 1.25 us  [send(): return lax.ppermute(value, 'sfc', pairs)]
    pallas_call x0 -> x2, Pallas kernels: none -> 20.2 us  [the longest x1 18.5 us: shards(): pl.pallas_call(functools.partial(cycles_kernel, depth, edge, tile), out_s...]
    reshape x4 -> x0, local copies, waits for them, and re-layouts: 19.3 us -> none  [the longest x2 11.2 us: restrict(): blocks = field.reshape(planes // 2, 2, half, 2, half, 2)]
    all_to_all x0 -> x1, blocking collectives: none -> 17.1 us  [shards(): sums = lax.all_to_all(sums, 'sfc', 0, 0, tiled=True)]
    all_gather x0 -> x1, blocking collectives: none -> 7.29 us  [shards(): gathered = lax.all_gather(cells, 'grp', axis=0, tiled=False)]
    reduce_sum x4 -> x0, other arithmetic: 6.74 us -> none  [the longest x2 5.2 us: restrict(): jnp.sum(blocks, axis=(1, 3, 5)).reshape(planes // 2, half * half)]
  transfers between devices with their start and end apart: 44 -> 4, of which waited for: 15 -> 1; matrix products, arithmetic and copies ran while one was open for 1% -> 2% of each run, Pallas kernels for 0% -> 0%
where the time goes in v1:
time: 62.2 us; the launch traced here: 61.8 us
  blocking collectives  24.4 us (39%)
  Pallas kernels  20.2 us (32%)
  starting transfers between devices  10.5 us (17%)
  between operations  2.72 us (4%)
  other arithmetic  1.66 us (3%)
  waiting for transfers between devices  1.25 us (2%)
  local copies, waits for them, and re-layouts  1.06 us (2%)
    pallas_call x1, Pallas kernels, shards(): pl.pallas_call(functools.partial(cycles_kernel, depth, edge, tile), out_s...  18.5 us
    all_to_all x1, blocking collectives, shards(): sums = lax.all_to_all(sums, 'sfc', 0, 0, tiled=True)  17.1 us
    ppermute x4, starting transfers between devices, send(): return lax.ppermute(value, 'sfc', pairs)  10.5 us
    all_gather x1, blocking collectives, shards(): gathered = lax.all_gather(cells, 'grp', axis=0, tiled=False)  7.29 us
    pallas_call x1, Pallas kernels, shards(): pl.pallas_call(finish_kernel, out_shape=[block] * 3, in_specs=[vmem] * 5,...  1.75 us
    ppermute x4, waiting for transfers between devices, send(): return lax.ppermute(value, 'sfc', pairs)  1.25 us
  transfers between devices with their start and end apart: 4, of which 1 were waited for; matrix products, arithmetic and copies ran while one was open for 2% of the time, Pallas kernels for 0%

profile of v1, /device:TPU:0, one launch (start us, length us, event | category | flops | bytes accessed | tf_op | source)
XLA Modules:
  0.0 61.8 jit_solution(5870765672267979354)
XLA Ops:
  1.3 0.9 %bitcast_select_fusion.r_ref = f32[64,256]{1,0:T(8,128)S(1)} fusion(f32[4,16,256]{2,1,0:T(8,128)} %param.2, pred[64]{0:T(512)(128)(4,1)S(1)} %iota_compare_fusion), kind=kLoop, calls=%fused_computation.1 | loop fusion | flops 16384 | bytes 131136 | tf_op jit(solution)/shard_map/jit(_where)/select_n | solution.py:233
  2.2 0.0 copy-start
  2.2 5.1 %collective-permute-start.3 = (f32[8,256]{1,0:T(8,128)S(1)}, f32[8,256]{1,0:T(8,128)S(1)}, u32[]{:S(2)}, u32[]{:S(2)}) collective-permute-start(f32[8,256]{1,0:T(8,128)S(1)} %get-tuple-element.17), channel_id=1, source_target_pairs={{0,24},{4,28},{8,0},{12,4},{16,8},{20,12},{24,16},{28,20},{1,25},{... | collective-permute-start | bytes 24584 | tf_op jit(solution)/shard_map/ppermute | solution.py:221
  7.4 0.0 collective-permute-start.2
  7.4 0.0 copy-start.1
  7.4 1.5 %collective-permute-start = (f32[32,256]{1,0:T(8,128)S(1)}, f32[32,256]{1,0:T(8,128)S(1)}, u32[]{:S(2)}, u32[]{:S(2)}) collective-permute-start(f32[32,256]{1,0:T(8,128)S(1)} %concatenate.13), channel_id=1, source_target_pairs={{0,4},{4,8},{8,12},{12,16},{16,20},{20,24},{24,28},{28,0},{1,5},{5... | collective-permute-start | bytes 98312 | tf_op jit(solution)/shard_map/ppermute | solution.py:221
  8.9 0.0 copy-done.1
  9.0 0.1 slice_select_fusion
  9.0 3.8 %collective-permute-start.1 = (f32[32,256]{1,0:T(8,128)S(1)}, f32[32,256]{1,0:T(8,128)S(1)}, u32[]{:S(2)}, u32[]{:S(2)}) collective-permute-start(f32[32,256]{1,0:T(8,128)S(1)} %slice_select_fusion), channel_id=1, source_target_pairs={{0,28},{4,0},{8,4},{12,8},{16,12},{20,16},{24,20},{28,24},{1,29},{... | collective-permute-start | bytes 98312 | tf_op jit(solution)/shard_map/ppermute | solution.py:221
  12.9 1.2 %collective-permute-done = f32[32,256]{1,0:T(8,128)S(1)} collective-permute-done((f32[32,256]{1,0:T(8,128)S(1)}, f32[32,256]{1,0:T(8,128)S(1)}, u32[]{:S(2)}, u32[]{:S(2)}) %collective-permute-start) | collective-permute-done | bytes 32800 | tf_op jit(solution)/shard_map/ppermute | solution.py:221
  14.1 0.5 slice.33
  15.3 0.0 collective-permute-done.2
  15.3 0.0 copy-done
  15.3 0.0 collective-permute-done.1
  15.4 0.5 slice.35
  16.5 0.0 collective-permute-done.3
  16.6 7.3 %all-gather = f32[448,256]{1,0:T(8,128)} all-gather(f32[112,256]{1,0:T(8,128)S(1)} %constant_dynamic-update-slice_fusion), channel_id=2, replica_groups=mesh['sfc'=8,'grp'=4] {'grp'}, dimensions={0}, use_global_device_ids=true | all-gather | bytes 573440 | tf_op jit(solution)/shard_map/all_gather | solution.py:263
  23.9 0.6 %pad_add_fusion.scalars = s32[4]{0:T(128)} fusion(s32[1]{0:T(128)} %bitcast.7, s32[1]{0:T(128)} %bitcast.6, s32[1]{0:T(128)} %bitcast.4, s32[1]{0:T(128)S(6)} %copy.9), kind=kLoop, calls=%fused_computation.14 | loop fusion | flops 12 | bytes 32 | tf_op jit(solution)/shard_map/stack | solution.py:262
  24.5 18.5 %shard_map.49 = (f32[64,256]{1,0:T(8,128)}, f32[64,256]{1,0:T(8,128)}, f32[64,256]{1,0:T(8,128)}, f32[64,128]{1,0:T(8,128)}) custom-call(s32[4]{0:T(128)} %pad_add_fusion.scalars, f32[4,112,256]{2,1,0:T(8,128)} %bitcast.15), custom_call_target="tpu_custom_call" | custom-call | tf_op jit(solution)/shard_map/pallas_call | solution.py:268
  43.0 17.1 %all_to_all.11 = f32[8,8,128]{2,1,0:T(8,128)} all-to-all(f32[8,8,128]{2,1,0:T(8,128)} %bitcast.17), channel_id=1, replica_groups=mesh['sfc'=8,'grp'=4] {'sfc'}, dimensions={0} | all-to-all | bytes 65536 | tf_op jit(solution)/shard_map/all_to_all | solution.py:275
  60.1 1.8 %shard_map.50 = (f32[64,256]{1,0:T(8,128)}, f32[64,256]{1,0:T(8,128)}, f32[64,256]{1,0:T(8,128)}) custom-call(f32[64,128]{1,0:T(8,128)} %bitcast.16, f32[64,256]{1,0:T(8,128)} %copy-done, f32[64,256]{1,0:T(8,128)} %get-tuple-element.11.z_ref, f32[64,256]{1,0:T(8,128)} %get-tuple-element.12.image_ref, f32[64,256]{1,0:T(8,128)} %get-tuple-element.13.again_ref), custom_call_target="tpu_custom_call" | custom-call | tf_op jit(solution)/shard_map/pallas_call | solution.py:276
  (9 shorter events, 0.1 us)
Async XLA Ops:
  2.2 13.1 %copy-start = (f32[64,256]{1,0:T(8,128)}, f32[64,256]{1,0:T(8,128)S(1)}, u32[]{:S(2)}) copy-start(f32[64,256]{1,0:T(8,128)S(1)} %bitcast_select_fusion.r_ref) | copy-start | bytes 196612
  2.2 14.3 %collective-permute-start.3 = (f32[8,256]{1,0:T(8,128)S(1)}, f32[8,256]{1,0:T(8,128)S(1)}, u32[]{:S(2)}, u32[]{:S(2)}) collective-permute-start(f32[8,256]{1,0:T(8,128)S(1)} %get-tuple-element.17), channel_id=1, source_target_pairs={{0,24},{4,28},{8,0},{12,4},{16,8},{20,12},{24,16},{28,20},{1,25},{... | collective-permute-start | bytes 24584 | tf_op jit(solution)/shard_map/ppermute | solution.py:221
  7.4 7.9 %collective-permute-start.2 = (f32[8,256]{1,0:T(8,128)S(1)}, f32[8,256]{1,0:T(8,128)S(1)}, u32[]{:S(2)}, u32[]{:S(2)}) collective-permute-start(f32[8,256]{1,0:T(8,128)S(1)} %get-tuple-element.18), channel_id=1, source_target_pairs={{0,8},{4,12},{8,16},{12,20},{16,24},{20,28},{24,0},{28,4},{1,9},{5... | collective-permute-start | bytes 24584 | tf_op jit(solution)/shard_map/ppermute | solution.py:221
  7.4 1.6 %copy-start.1 = (pred[32]{0:T(512)(128)(4,1)S(1)}, pred[32]{0:T(512)(128)(4,1)}, u32[]{:S(2)}) copy-start(pred[32]{0:T(512)(128)(4,1)} %constant.39.clone.1) | copy-start | bytes 100
  7.4 6.7 %collective-permute-start = (f32[32,256]{1,0:T(8,128)S(1)}, f32[32,256]{1,0:T(8,128)S(1)}, u32[]{:S(2)}, u32[]{:S(2)}) collective-permute-start(f32[32,256]{1,0:T(8,128)S(1)} %concatenate.13), channel_id=1, source_target_pairs={{0,4},{4,8},{8,12},{12,16},{16,20},{20,24},{24,28},{28,0},{1,5},{5... | collective-permute-start | bytes 98312 | tf_op jit(solution)/shard_map/ppermute | solution.py:221
  9.0 6.3 %collective-permute-start.1 = (f32[32,256]{1,0:T(8,128)S(1)}, f32[32,256]{1,0:T(8,128)S(1)}, u32[]{:S(2)}, u32[]{:S(2)}) collective-permute-start(f32[32,256]{1,0:T(8,128)S(1)} %slice_select_fusion), channel_id=1, source_target_pairs={{0,28},{4,0},{8,4},{12,8},{16,12},{20,16},{24,20},{28,24},{1,29},{... | collective-permute-start | bytes 98312 | tf_op jit(solution)/shard_map/ppermute | solution.py:221

commit v2 on v1

--- a/solution.py
+++ b/solution.py
@@ -13,6 +13,7 @@
 OMEGA = 2.0 / 3.0
 LANES = 128
 ROWS = 8
+SPAN = 16
 
 
 def halo_depth():
@@ -29,7 +30,7 @@
     return pltpu.roll(value, amount % LANES, 1)
 
 
-def neighbours(value, reach, edge):
+def neighbours(value, next_row, last_row, reach, edge):
     rows = value.shape[0]
     lane = lax.broadcasted_iota(jnp.int32, value.shape, 1)
     row = lax.broadcasted_iota(jnp.int32, value.shape, 0)
@@ -37,12 +38,12 @@
     hop = reach * edge
     up = jnp.where(column < edge - reach, shift_lanes(value, -reach), 0.0)
     down = jnp.where(column >= reach, shift_lanes(value, reach), 0.0)
-    ahead = shift_lanes(value, -hop)
-    over = jnp.where(row == rows - 1, 0.0, pltpu.roll(ahead, rows - 1, 0))
-    north = jnp.where(lane < LANES - hop, ahead, over)
-    behind = shift_lanes(value, hop)
-    under = jnp.where(row == 0, 0.0, pltpu.roll(behind, 1, 0))
-    south = jnp.where(lane >= hop, behind, under)
+    low = lane < hop
+    ahead = jnp.where(low, next_row, value)
+    north = shift_lanes(jnp.where(low & (row == rows - 1), 0.0, ahead), -hop)
+    high = lane >= LANES - hop
+    behind = jnp.where(high, last_row, value)
+    south = shift_lanes(jnp.where(high & (row == 0), 0.0, behind), hop)
     return (up + down) + (north + south)
 
 
@@ -55,26 +56,35 @@
 
 
 def cycles_kernel(
-    depth, edge, tile, scalars, cells, z_out, image_out, again_out, sums_out,
+    depth, edge, tile, scalars, back_mark, front_mark, cells, z_out, image_out, again_out, sums_out,
     r_ref, z_ref, t_ref, image_ref, c_ref, e_ref, f_ref,
 ):
     groups, padded, width = cells.shape
     planes = padded - 2 * depth
     parts = width // LANES
-    count, above, under, group = scalars[0], scalars[1], scalars[2], scalars[3]
-    first = (depth - above) // ROWS
+    count, group, index, peers = scalars[0], scalars[1], scalars[2], scalars[3]
+    back_thin = jnp.max(back_mark[...]) < 1.5
+    front_thin = jnp.max(front_mark[...]) < 1.5
+    above = jnp.where((index == 1) & back_thin, edge, depth)
+    above = jnp.where(index == 0, 0, above)
+    under = jnp.where((index == peers - 2) & front_thin, edge, depth)
+    under = jnp.where(index == peers - 1, 0, under)
     live_end = depth + count * edge
-    last = (live_end + under) // ROWS
-    own_first, own_last = depth // ROWS, live_end // ROWS
+    first, last = depth - above, live_end + under
     step = OMEGA / 6.0
     coarse_step = OMEGA / 1.5
-    half_rows = ROWS // 2
-
-    def at(plane):
-        return pl.ds(pl.multiple_of((plane + 1) * tile, ROWS), tile)
-
-    for ref in (r_ref, z_ref, t_ref, image_ref, c_ref, e_ref, f_ref):
-        ref[...] = jnp.zeros(ref.shape, jnp.float32)
+
+    def at(plane, shift=0):
+        start = pl.multiple_of((plane + 1) * tile, ROWS)
+        return pl.ds(start + shift if shift else start, tile)
+
+    zero = jnp.zeros((tile, LANES), jnp.float32)
+    for ref in (r_ref, z_ref, t_ref, image_ref):
+        ref[at(first - 1), :] = zero
+        ref[at(last), :] = zero
+    for ref in (c_ref, e_ref, f_ref):
+        ref[at(first // 2 - 1), :] = zero
+        ref[at(last // 2), :] = zero
 
     for block in range(padded // ROWS):
         low = block * ROWS
@@ -84,71 +94,85 @@
             lanes = slice(part % parts * LANES, (part % parts + 1) * LANES)
             r_ref[rows, :] = cells[part // parts, low : low + ROWS, lanes]
 
-    def sweep(begin, end, size, reach, source, emit):
+    def sweep(reach, scale, around_of, emit):
+        low = jnp.maximum(first, depth - reach) // scale
+        high = jnp.minimum(last, live_end + reach) // scale
+        size = SPAN // scale
+
         def body(block, carry):
-            base = block * size
-            window = [source[at(base + k), :] for k in range(-1, size + 1)]
-            applied = []
+            base = jnp.minimum(low + block * size, high - size)
+            window = [around_of[at(base + k), :] for k in range(-1, size + 1)]
+            around = []
             for k in range(size):
-                middle = window[k + 1]
-                around = neighbours(middle, reach, edge) + (window[k] + window[k + 2])
-                applied.append(6.0 * middle - around)
-            emit(base, window[1:-1], applied)
+                flat = neighbours(
+                    window[k + 1],
+                    around_of[at(base + k, 1), :],
+                    around_of[at(base + k, -1), :],
+                    scale,
+                    edge,
+                )
+                around.append(flat + (window[k] + window[k + 2]))
+            emit(base, window[1:-1], around)
             return carry
 
-        lax.fori_loop(begin, end, body, 0)
-
-    def cycle(rhs):
-        def first_sweep(base, middle, applied):
-            for k in range(ROWS):
-                z_ref[at(base + k), :] = step * (2.0 * middle[k] - step * applied[k])
-
-        sweep(first, last, ROWS, 1, rhs, first_sweep)
-
-        def coarsen(base, middle, applied):
-            for k in range(half_rows):
-                pair = (rhs[at(base + 2 * k), :] - applied[2 * k]) + (
-                    rhs[at(base + 2 * k + 1), :] - applied[2 * k + 1]
-                )
+        lax.fori_loop(0, (high - low + size - 1) // size, body, 0)
+
+    def cycle(rhs, reach):
+        smooth_reach = reach + POST_SWEEPS + (reach + POST_SWEEPS) % 2
+        coarse_reach = smooth_reach + 2 * (COARSE_SWEEPS - 1)
+
+        def first_sweep(base, middle, around):
+            for k in range(SPAN):
+                z_ref[at(base + k), :] = (step * (2.0 - OMEGA)) * middle[k] + (
+                    step * step
+                ) * around[k]
+
+        sweep(coarse_reach + 1, 1, rhs, first_sweep)
+
+        def coarsen(base, middle, around):
+            defect = [rhs[at(base + k), :] - 6.0 * middle[k] + around[k] for k in range(SPAN)]
+            for k in range(SPAN // 2):
+                pair = defect[2 * k] + defect[2 * k + 1]
                 c_ref[at(base // 2 + k), :] = 0.125 * block_sum(pair, edge)
 
-        sweep(first, last, ROWS, 1, z_ref, coarsen)
-
-        def coarse_start(base, middle, applied):
-            for k in range(half_rows):
-                e_ref[at(base + k), :] = coarse_step * (
-                    2.0 * middle[k] - (0.25 * coarse_step) * applied[k]
-                )
-
-        sweep(first, last, half_rows, 2, c_ref, coarse_start)
+        sweep(coarse_reach, 1, z_ref, coarsen)
+
+        keep = 1.0 - 1.5 * coarse_step
+        spread = 0.25 * coarse_step
+
+        def coarse_start(base, middle, around):
+            for k in range(SPAN // 2):
+                e_ref[at(base + k), :] = (coarse_step * (1.0 + keep)) * middle[k] + (
+                    spread * coarse_step
+                ) * around[k]
+
+        sweep(coarse_reach - 2, 2, c_ref, coarse_start)
         held, spare = e_ref, f_ref
         for index in range(COARSE_SWEEPS - 2):
             final = index == COARSE_SWEEPS - 3
 
-            def coarse_next(base, middle, applied, spare=spare, final=final):
-                for k in range(half_rows):
-                    value = middle[k] + coarse_step * (
-                        c_ref[at(base + k), :] - 0.25 * applied[k]
-                    )
+            def coarse_next(base, middle, around, spare=spare, final=final):
+                for k in range(SPAN // 2):
+                    value = (keep * middle[k] + spread * around[k]) + coarse_step * c_ref[at(base + k), :]
                     if final:
                         for fine in (2 * (base + k), 2 * (base + k) + 1):
-                            z_ref[at(fine), :] = z_ref[at(fine), :] + value
+                            t_ref[at(fine), :] = z_ref[at(fine), :] + value
                     else:
                         spare[at(base + k), :] = value
 
-            sweep(first, last, half_rows, 2, held, coarse_next)
+            sweep(coarse_reach - 4 - 2 * index, 2, held, coarse_next)
             held, spare = spare, held
 
-        here, there = z_ref, t_ref
+        here, there = t_ref, z_ref
         for index in range(POST_SWEEPS):
 
-            def smooth(base, middle, applied, there=there):
-                for k in range(ROWS):
-                    there[at(base + k), :] = middle[k] + step * (
-                        rhs[at(base + k), :] - applied[k]
+            def smooth(base, middle, around, there=there):
+                for k in range(SPAN):
+                    there[at(base + k), :] = (1.0 - OMEGA) * middle[k] + step * (
+                        rhs[at(base + k), :] + around[k]
                     )
 
-            sweep(first, last, ROWS, 1, here, smooth)
+            sweep(reach + POST_SWEEPS - 1 - index, 1, here, smooth)
             here, there = there, here
         return here
 
@@ -161,16 +185,18 @@
                 rows = slice(block * ROWS, (block + 1) * ROWS)
                 out[rows, lanes] = jnp.where(block * ROWS < count * edge, value, 0.0)
 
-    zero = jnp.zeros((tile, LANES), jnp.float32)
-    result = cycle(r_ref)
+    again_reach = 2 * (POST_SWEEPS - POST_SWEEPS // 2) + 2 * (COARSE_SWEEPS - 1) + PRE_SWEEPS
+    result = cycle(r_ref, again_reach + 1)
     store(result, z_out)
 
-    def to_image(base, middle, applied):
-        for k in range(ROWS):
-            image_ref[at(base + k), :] = applied[k]
-
-    sweep(first, last, ROWS, 1, result, to_image)
+    def to_image(base, middle, around):
+        for k in range(SPAN):
+            image_ref[at(base + k), :] = 6.0 * middle[k] - around[k]
+
+    sweep(again_reach, 1, result, to_image)
     store(image_ref, image_out)
+
+    own_first, own_last = depth // ROWS, live_end // ROWS
 
     def first_sums(block, carry):
         rz, curv = carry
@@ -181,7 +207,7 @@
         return rz, curv
 
     rz, curv = lax.fori_loop(own_first, own_last, first_sums, (zero, zero))
-    again = cycle(image_ref)
+    again = cycle(image_ref, 0)
     store(again, again_out)
 
     def last_sum(block, mixed):
@@ -239,9 +265,9 @@
     from_front = send(jnp.concatenate([own[:depth], mark], axis=0), -1)
     from_far_back = send(far_tail, 2)
     from_far_front = send(own[:far], -2)
-    back_count, front_count = from_back[depth, 0], from_front[depth, 0]
+    back_mark, front_mark = from_back[depth:], from_front[depth:]
     index = lax.axis_index("sfc")
-    back_thin, front_thin = back_count < 1.5, front_count < 1.5
+    back_thin, front_thin = back_mark[:1] < 1.5, front_mark[:1] < 1.5
     back, front = index > 0, index < peers - 1
     far_back = jnp.where(index > 1, from_far_back, 0.0)
     far_front = jnp.where(index < peers - 2, from_far_front, 0.0)
@@ -255,11 +281,7 @@
         ],
         axis=0,
     )
-    above = jnp.where((index == 1) & back_thin, edge, depth)
-    above = jnp.where(index == 0, 0, above)
-    under = jnp.where((index == peers - 2) & front_thin, edge, depth)
-    under = jnp.where(index == peers - 1, 0, under)
-    scalars = jnp.stack([count, above, under, lax.axis_index("grp")]).astype(jnp.int32)
+    scalars = jnp.stack([count, lax.axis_index("grp"), index, jnp.int32(peers)]).astype(jnp.int32)
     gathered = lax.all_gather(cells, "grp", axis=0, tiled=False)
     fine = pltpu.VMEM(((planes + 2 * depth + 2) * tile, LANES), jnp.float32)
     coarse = pltpu.VMEM(((planes // 2 + depth + 2) * tile, LANES), jnp.float32)
@@ -268,10 +290,10 @@
     z, image, again, sums = pl.pallas_call(
         functools.partial(cycles_kernel, depth, edge, tile),
         out_shape=[block, block, block, jax.ShapeDtypeStruct((peers * ROWS, LANES), jnp.float32)],
-        in_specs=[pl.BlockSpec(memory_space=pltpu.SMEM), vmem],
+        in_specs=[pl.BlockSpec(memory_space=pltpu.SMEM)] + [vmem] * 3,
         out_specs=[vmem] * 4,
         scratch_shapes=[fine, fine, fine, fine, coarse, coarse, coarse],
-    )(scalars, gathered)
+    )(scalars, back_mark, front_mark, gathered)
     sums = lax.all_to_all(sums, "sfc", 0, 0, tiled=True)
     outs = pl.pallas_call(
         finish_kernel,

time: 62.2 us -> 54.6 us (0.88)
  blocking collectives: 24.4 us -> 17.9 us
  waiting for transfers between devices: 1.25 us -> 5.99 us
  Pallas kernels: 20.2 us -> 15.6 us
  between operations: 2.72 us -> 1.36 us
  other arithmetic: 1.66 us -> 2.87 us
    all_to_all x1, blocking collectives: 17.1 us -> 10.6 us  [shards(): sums = lax.all_to_all(sums, 'sfc', 0, 0, tiled=True)]
    ppermute x4, waiting for transfers between devices: 1.25 us -> 5.99 us  [send(): return lax.ppermute(value, 'sfc', pairs)]
    pallas_call x1, Pallas kernels: 18.5 us -> 13.8 us  [shards(): pl.pallas_call(functools.partial(cycles_kernel, depth, edge, tile), out_s...]
    slice x2 -> x0, local copies, waits for them, and re-layouts: 1.02 us -> none  [shards(): back_count, front_count = (from_back[depth, 0], from_front[depth, 0])]
    unnamed x5, local copies, waits for them, and re-layouts: 0.01 us -> 0.66 us
  transfers between devices with their start and end apart: 4 -> 4, of which waited for: 1 -> 1; matrix products, arithmetic and copies ran while one was open for 2% -> 3% of each run, Pallas kernels for 0% -> 0%
where the time goes in v2:
time: 54.6 us; the launch traced here: 54.3 us
  blocking collectives  17.9 us (33%)
  Pallas kernels  15.6 us (29%)
  starting transfers between devices  9.94 us (18%)
  waiting for transfers between devices  5.99 us (11%)
  other arithmetic  2.87 us (5%)
  between operations  1.36 us (2%)
  local copies, waits for them, and re-layouts  0.69 us (1%)
    pallas_call x1, Pallas kernels, shards(): pl.pallas_call(functools.partial(cycles_kernel, depth, edge, tile), out_s...  13.8 us
    all_to_all x1, blocking collectives, shards(): sums = lax.all_to_all(sums, 'sfc', 0, 0, tiled=True)  10.6 us
    ppermute x4, starting transfers between devices, send(): return lax.ppermute(value, 'sfc', pairs)  9.94 us
    all_gather x1, blocking collectives, shards(): gathered = lax.all_gather(cells, 'grp', axis=0, tiled=False)  7.28 us
    ppermute x4, waiting for transfers between devices, send(): return lax.ppermute(value, 'sfc', pairs)  5.99 us
    pallas_call x1, Pallas kernels, shards(): pl.pallas_call(finish_kernel, out_shape=[block] * 3, in_specs=[vmem] * 5,...  1.75 us
  transfers between devices with their start and end apart: 4, of which 1 were waited for; matrix products, arithmetic and copies ran while one was open for 3% of the time, Pallas kernels for 0%

profile of v2, /device:TPU:0, one launch (start us, length us, event | category | flops | bytes accessed | tf_op | source)
XLA Modules:
  0.0 54.3 jit_solution(15056827400194032901)
XLA Ops:
  1.3 0.9 %bitcast_select_fusion.r_ref = f32[64,256]{1,0:T(8,128)S(1)} fusion(f32[4,16,256]{2,1,0:T(8,128)} %param.2, pred[64]{0:T(512)(128)(4,1)S(1)} %iota_compare_fusion), kind=kLoop, calls=%fused_computation.1 | loop fusion | flops 16384 | bytes 131136 | tf_op jit(solution)/shard_map/jit(_where)/select_n | solution.py:259
  2.2 0.0 copy-start
  2.2 5.1 %collective-permute-start.3 = (f32[8,256]{1,0:T(8,128)S(1)}, f32[8,256]{1,0:T(8,128)S(1)}, u32[]{:S(2)}, u32[]{:S(2)}) collective-permute-start(f32[8,256]{1,0:T(8,128)S(1)} %get-tuple-element.17), channel_id=1, source_target_pairs={{0,24},{4,28},{8,0},{12,4},{16,8},{20,12},{24,16},{28,20},{1,25},{... | collective-permute-start | bytes 24584 | tf_op jit(solution)/shard_map/ppermute | solution.py:247
  7.4 0.0 collective-permute-start.2
  7.4 0.0 copy-start.1
  7.4 0.7 %copy-done.1 = pred[32]{0:T(512)(128)(4,1)S(1)} copy-done((pred[32]{0:T(512)(128)(4,1)S(1)}, pred[32]{0:T(512)(128)(4,1)}, u32[]{:S(2)}) %copy-start.1) | copy-done | bytes 56
  8.0 0.1 slice_select_fusion
  8.1 4.7 %collective-permute-start.1 = (f32[32,256]{1,0:T(8,128)S(1)}, f32[32,256]{1,0:T(8,128)S(1)}, u32[]{:S(2)}, u32[]{:S(2)}) collective-permute-start(f32[32,256]{1,0:T(8,128)S(1)} %slice_select_fusion), channel_id=1, source_target_pairs={{0,28},{4,0},{8,4},{12,8},{16,12},{20,16},{24,20},{28,24},{1,29},{... | collective-permute-start | bytes 98312 | tf_op jit(solution)/shard_map/ppermute | solution.py:247
  12.9 0.1 collective-permute-start
  12.9 0.6 %pad_add_fusion.scalars = s32[4]{0:T(128)} fusion(s32[1]{0:T(128)} %constant.12.clone.1, s32[1]{0:T(128)} %bitcast.1, s32[1]{0:T(128)} %bitcast, s32[1]{0:T(128)S(6)} %copy.9), kind=kLoop, calls=%fused_computation.16 | loop fusion | flops 12 | bytes 32 | tf_op jit(solution)/shard_map/stack | solution.py:284
  13.6 6.0 %collective-permute-done = f32[32,256]{1,0:T(8,128)S(1)} collective-permute-done((f32[32,256]{1,0:T(8,128)S(1)}, f32[32,256]{1,0:T(8,128)S(1)}, u32[]{:S(2)}, u32[]{:S(2)}) %collective-permute-start) | collective-permute-done | bytes 32800 | tf_op jit(solution)/shard_map/ppermute | solution.py:247
  19.6 0.0 collective-permute-done.2
  19.6 0.6 %constant_dynamic-update-slice_fusion.2 = (f32[112,256]{1,0:T(8,128)S(1)}, f32[8,256]{1,0:T(8,128)}) fusion(f32[32,256]{1,0:T(8,128)S(1)} %collective-permute-done, f32[8,256]{1,0:T(8,128)S(1)} %collective-permute-done.2, pred[]{:T(512)S(6)} %gt.7, pred[256]{0:T(512)(128)(4,1)S(1)} %compare_reduce_fusion.1, pred[]{:T(512)S(6)} %gt.6), kind=kLoop, calls=%fused_computation.9 | loop fusion | flops 6143 | bytes 41218
  20.2 0.0 copy-done
  20.2 0.0 collective-permute-done.1
  20.2 0.0 collective-permute-done.3
  20.2 0.6 %constant_dynamic-update-slice_fusion = (f32[112,256]{1,0:T(8,128)S(1)}, f32[8,256]{1,0:T(8,128)}) fusion(f32[112,256]{1,0:T(8,128)S(1)} %fusion, f32[32,256]{1,0:T(8,128)S(1)} %collective-permute-done.1, f32[8,256]{1,0:T(8,128)S(1)} %collective-permute-done.3, pred[]{:T(512)S(6)} %lt.36, pred[256]{0:T(512)(128)(4,1)S(1)} %compare_reduce_fusion, pred[]{:T(512)S(6)} %lt.34), kind=kLoop, calls=%fused_computation.7 | loop fusion | flops 6144 | bytes 41474 | tf_op jit(solution)/shard_map/concatenate | solution.py:274
  20.8 7.3 %all-gather = f32[448,256]{1,0:T(8,128)} all-gather(f32[112,256]{1,0:T(8,128)S(1)} %get-tuple-element.19), channel_id=2, replica_groups=mesh['sfc'=8,'grp'=4] {'grp'}, dimensions={0}, use_global_device_ids=true | all-gather | bytes 573440 | tf_op jit(solution)/shard_map/all_gather | solution.py:285
  28.1 13.8 %shard_map.49 = (f32[64,256]{1,0:T(8,128)}, f32[64,256]{1,0:T(8,128)}, f32[64,256]{1,0:T(8,128)}, f32[64,128]{1,0:T(8,128)}) custom-call(s32[4]{0:T(128)} %pad_add_fusion.scalars, f32[8,256]{1,0:T(8,128)} %get-tuple-element.22.back_mark, f32[8,256]{1,0:T(8,128)} %get-tuple-element.20.front_mark, f32[4,112,256]{2,1,0:T(8,128)} %bitcast.12), custom_call_target="tpu_custom_call" | custom-call | tf_op jit(solution)/shard_map/pallas_call | solution.py:290
  41.9 10.6 %all_to_all.11 = f32[8,8,128]{2,1,0:T(8,128)} all-to-all(f32[8,8,128]{2,1,0:T(8,128)} %bitcast.14), channel_id=1, replica_groups=mesh['sfc'=8,'grp'=4] {'sfc'}, dimensions={0} | all-to-all | bytes 65536 | tf_op jit(solution)/shard_map/all_to_all | solution.py:297
  52.5 1.8 %shard_map.50 = (f32[64,256]{1,0:T(8,128)}, f32[64,256]{1,0:T(8,128)}, f32[64,256]{1,0:T(8,128)}) custom-call(f32[64,128]{1,0:T(8,128)} %bitcast.13, f32[64,256]{1,0:T(8,128)} %copy-done, f32[64,256]{1,0:T(8,128)} %get-tuple-element.11.z_ref, f32[64,256]{1,0:T(8,128)} %get-tuple-element.12.image_ref, f32[64,256]{1,0:T(8,128)} %get-tuple-element.13.again_ref), custom_call_target="tpu_custom_call" | custom-call | tf_op jit(solution)/shard_map/pallas_call | solution.py:298
  (9 shorter events, 0.1 us)
Async XLA Ops:
  2.2 18.0 %copy-start = (f32[64,256]{1,0:T(8,128)}, f32[64,256]{1,0:T(8,128)S(1)}, u32[]{:S(2)}) copy-start(f32[64,256]{1,0:T(8,128)S(1)} %bitcast_select_fusion.r_ref) | copy-start | bytes 196612
  2.2 18.0 %collective-permute-start.3 = (f32[8,256]{1,0:T(8,128)S(1)}, f32[8,256]{1,0:T(8,128)S(1)}, u32[]{:S(2)}, u32[]{:S(2)}) collective-permute-start(f32[8,256]{1,0:T(8,128)S(1)} %get-tuple-element.17), channel_id=1, source_target_pairs={{0,24},{4,28},{8,0},{12,4},{16,8},{20,12},{24,16},{28,20},{1,25},{... | collective-permute-start | bytes 24584 | tf_op jit(solution)/shard_map/ppermute | solution.py:247
  7.4 12.2 %collective-permute-start.2 = (f32[8,256]{1,0:T(8,128)S(1)}, f32[8,256]{1,0:T(8,128)S(1)}, u32[]{:S(2)}, u32[]{:S(2)}) collective-permute-start(f32[8,256]{1,0:T(8,128)S(1)} %get-tuple-element.18), channel_id=1, source_target_pairs={{0,8},{4,12},{8,16},{12,20},{16,24},{20,28},{24,0},{28,4},{1,9},{5... | collective-permute-start | bytes 24584 | tf_op jit(solution)/shard_map/ppermute | solution.py:247
  7.4 0.7 %copy-start.1 = (pred[32]{0:T(512)(128)(4,1)S(1)}, pred[32]{0:T(512)(128)(4,1)}, u32[]{:S(2)}) copy-start(pred[32]{0:T(512)(128)(4,1)} %constant.33.clone.1) | copy-start | bytes 100
  8.1 12.1 %collective-permute-start.1 = (f32[32,256]{1,0:T(8,128)S(1)}, f32[32,256]{1,0:T(8,128)S(1)}, u32[]{:S(2)}, u32[]{:S(2)}) collective-permute-start(f32[32,256]{1,0:T(8,128)S(1)} %slice_select_fusion), channel_id=1, source_target_pairs={{0,28},{4,0},{8,4},{12,8},{16,12},{20,16},{24,20},{28,24},{1,29},{... | collective-permute-start | bytes 98312 | tf_op jit(solution)/shard_map/ppermute | solution.py:247
  12.9 6.7 %collective-permute-start = (f32[32,256]{1,0:T(8,128)S(1)}, f32[32,256]{1,0:T(8,128)S(1)}, u32[]{:S(2)}, u32[]{:S(2)}) collective-permute-start(f32[32,256]{1,0:T(8,128)S(1)} %concatenate.13), channel_id=1, source_target_pairs={{0,4},{4,8},{8,12},{12,16},{16,20},{20,24},{24,28},{28,0},{1,5},{5... | collective-permute-start | bytes 98312 | tf_op jit(solution)/shard_map/ppermute | solution.py:247
